TPU v7x, 128 devices: a whole 4x4x4 slice. The times are simulated.
128 devices in a mesh: px: 8 (over y, x_lo), py: 16 (over z, x_hi, core).
Axes of the slice: x: 4 (x_hi: 2, x_lo: 2; x = x_hi * 2 + x_lo), y: 4, z: 4, core: 2. Of those that a mesh axis runs over, the one named last changes fastest.
Arguments:
- coefficients: bfloat16 [1536, 49152], P(('px', 'py')), may hold values from -6 to 6
- exponents: int32 [384, 3072], P(('px', 'py')), may hold values from -4 to 1
- right_side: float32 [128, 384, 1536], P('px', 'py'), may hold values from -18 to 18
Outputs:
- decoded: float32 [128, 384, 1536], P('px', 'py')
- residual: float32 [128, 384, 1536], P('px', 'py')
- rms: float32 [], replicated
All inputs are finite; a program needn't handle non-finite values.
Results may differ from a plain program's by a relative error of at most 0.0003.
Values may be sent and summed in bfloat16 or wider, within the bound.
A program may use at most 64 MiB of HBM per device.

v0:
```python
import functools

import jax
import jax.numpy as jnp
from jax import lax
from jax.sharding import Mesh
from jax.sharding import PartitionSpec as P

CX = 16
CY = 24
PX = ("px_0", "px_1")
PY = ("py_0", "py_1", "py_2")
PX_PY = ("px_0", "px_1", "py_0", "py_1", "py_2")


def with_halo(cells, sides, width):
    for axis, dim in sides:
        count = lax.axis_size(axis)
        ends = count - 1
        head = lax.slice_in_dim(cells, 0, width, axis=dim)
        tail = lax.slice_in_dim(cells, cells.shape[dim] - width, cells.shape[dim], axis=dim)
        cells = jnp.concatenate(
            [
                lax.ppermute(tail, axis, [(i, (i + 1) % count) for i in range(ends)]),
                cells,
                lax.ppermute(head, axis, [((i + 1) % count, i) for i in range(ends)]),
            ],
            axis=dim,
        )
    return cells


def one_axis_at_a_time(x, axes):
    return functools.reduce(lax.psum, axes, x)


def block_basis(width):
    rows = jnp.arange(width, dtype=jnp.int32)[:, None]
    cols = jnp.arange(width, dtype=jnp.int32)[None, :]
    frequency = (rows % 4).astype(jnp.float32)
    point = (cols % 4).astype(jnp.float32)
    weight = jnp.where(frequency == 0, jnp.sqrt(jnp.float32(0.25)), jnp.sqrt(jnp.float32(0.5)))
    entry = weight * jnp.cos(jnp.pi * (2.0 * point + 1.0) * frequency / 8.0)
    return jnp.where(rows // 4 == cols // 4, entry, 0.0)


def plane_table():
    across_x = block_basis(CX)
    across_y = block_basis(CY)
    return jnp.einsum("ux,vy->uvxy", across_x, across_y).reshape(CX * CY, CX * CY)


def spread_table():
    quarter_y = CY // 4
    blocks = jnp.arange(CX // 4 * quarter_y, dtype=jnp.int32)[:, None]
    cells = jnp.arange(CX * CY, dtype=jnp.int32)[None, :]
    same_x = cells // CY // 4 == blocks // quarter_y
    same_y = cells % CY // 4 == blocks % quarter_y
    return jnp.where(same_x & same_y, 1.0, 0.0).astype(jnp.float32)


def apply_plane(layers, table):
    return jnp.einsum(
        "zpc,cv->zpv", layers.astype(jnp.float32), table, precision=lax.Precision.HIGHEST
    )


def shards(coefficients, exponents, right_side):
    count_x = lax.axis_size(PX)
    count_y = lax.axis_size(PY)
    peers = count_x * count_y
    patch = CX * CY
    layer_count = coefficients.shape[0]
    block_layers = exponents.shape[0]
    table = plane_table()
    factor = jnp.exp2(exponents.astype(jnp.float32)).reshape(block_layers, peers, -1)
    spread = jnp.einsum("zpq,qc->zpc", factor, spread_table(), precision=lax.Precision.HIGHEST)
    spread = jnp.broadcast_to(spread[:, None], (block_layers, 4, peers, patch)).reshape(
        layer_count, peers, patch
    )
    scaled = (coefficients.astype(jnp.float32).reshape(layer_count, peers, patch) * spread).astype(
        jnp.bfloat16
    )
    received = lax.all_to_all(scaled, PX_PY, split_axis=1, concat_axis=1, tiled=True)
    arrived = apply_plane(received, table)
    stacked = arrived.transpose(1, 0, 2).reshape(-1, 128, patch)
    depth_table = block_basis(128)
    decoded = jnp.einsum(
        "nzq,zw->qnw", stacked, depth_table, precision=lax.Precision.HIGHEST
    ).reshape(CX, CY, -1)
    padded = with_halo(decoded, ((PX, 0), (PY, 1)), 1)
    padded = jnp.pad(padded, ((0, 0), (0, 0), (1, 1)))
    beside = padded[2:, 1:-1, 1:-1] + padded[:-2, 1:-1, 1:-1]
    beside = beside + padded[1:-1, 2:, 1:-1] + padded[1:-1, :-2, 1:-1]
    beside = beside + padded[1:-1, 1:-1, 2:] + padded[1:-1, 1:-1, :-2]
    residual = right_side - (6.0 * decoded - beside)
    local_sum = jnp.sum(residual * residual)
    total_sum = one_axis_at_a_time(local_sum, PX_PY)
    cell_count = decoded.shape[0] * decoded.shape[1] * decoded.shape[2] * count_x * count_y
    rms = jnp.sqrt(total_sum / cell_count + 1e-06)
    return (decoded, residual, rms)


def solution(mesh):
    finer = Mesh(mesh.devices.reshape(4, 2, 4, 2, 2), ("px_0", "px_1", "py_0", "py_1", "py_2"))
    placed = (P(PX_PY, None), P(PX_PY, None), P(PX, PY, None))
    return jax.shard_map(
        shards,
        mesh=finer,
        in_specs=placed,
        out_specs=(P(PX, PY, None), P(PX, PY, None), P()),
        check_vma=False,
    )
```

profile of v0, /device:TPU:1, one launch (start us, length us, event | category | flops | bytes accessed | tf_op | source)
XLA Modules:
  0.0 122.4 jit_solution(14215732069306532386)
XLA Ops:
  0.7 0.8 multiply_exponential_fusion
  1.7 1.6 %reshape.525 = f32[12,49152]{1,0:T(8,128)S(1)} convert(bf16[12,49152]{1,0:T(8,128)(2,1)} %param.3) | non-fusion elementwise | flops 589824 | bytes 3538944 | tf_op jit(solution)/shard_map/reshape | solution.py:81
  3.3 0.6 copy.34
  3.9 0.7 fusion.15
  4.6 0.3 fusion.1
  4.9 1.9 %copy.27 = bf16[12,128,384]{2,0,1:T(8,128)(2,1)} copy(bf16[12,128,384]{2,1,0:T(8,128)(2,1)S(1)} %fusion.1) | data formatting | bytes 2359296 | tf_op jit(solution)/shard_map/convert_element_type | solution.py:81
  6.7 11.9 %all-to-all-start = ((bf16[12,128,384]{2,0,1:T(8,128)(2,1)}), bf16[12,128,384]{2,0,1:T(8,128)(2,1)}, u32[]{:S(2)}, u32[]{:S(2)}) async-start(bf16[12,128,384]{2,0,1:T(8,128)(2,1)} %copy.27), calls=%async_computation | async-start | bytes 3145728 | tf_op jit(solution)/shard_map/all_to_all | solution.py:84
  19.0 0.3 multiply_bitcast_fusion
  19.3 2.3 %reshape.528 = f32[384,384,1]{1,0,2:T(8,128)} reshape(f32[16,24,16,24]{3,2,1,0:T(8,128)S(1)} %multiply_bitcast_fusion) | data formatting | bytes 1179648 | tf_op jit(solution)/shard_map/reshape | solution.py:50
  21.7 21.4 %all-to-all-done = bf16[12,128,384]{2,0,1:T(8,128)(2,1)} async-done(((bf16[12,128,384]{2,0,1:T(8,128)(2,1)}), bf16[12,128,384]{2,0,1:T(8,128)(2,1)}, u32[]{:S(2)}, u32[]{:S(2)}) %all-to-all-start) | async-done | bytes 1179680 | tf_op jit(solution)/shard_map/all_to_all | solution.py:84
  43.1 4.0 %convolution_bitcast_fusion.1 = f32[128,12,384]{2,0,1:T(8,128)S(1)} fusion(f32[384,384,1]{1,0,2:T(8,128)} %reshape.528, bf16[12,128,384]{2,0,1:T(8,128)(2,1)} %all-to-all-done), kind=kOutput, calls=%fused_computation.21 | convolution fusion | flops 2717908992 | bytes 4128768 | tf_op jit(solution)/shard_map/zpc,cv->zpv/dot_general | solution.py:63
  47.1 1.4 %copy.29 = f32[128,12,384]{2,1,0:T(8,128)S(1)} copy(f32[128,12,384]{2,0,1:T(8,128)S(1)} %convolution_bitcast_fusion.1) | data formatting | bytes 4718592 | tf_op jit(solution)/shard_map/transpose | solution.py:86
  48.5 1.5 %reshape.523 = f32[12,128,384]{2,1,0:T(8,128)} reshape(f32[128,12,384]{2,1,0:T(8,128)S(1)} %copy.29) | data formatting | bytes 4718592 | tf_op jit(solution)/shard_map/reshape | solution.py:86
  50.1 4.0 %convolution_bitcast_fusion = f32[384,12,128]{0,2,1:T(8,128)S(1)} fusion(f32[12,128,384]{2,1,0:T(8,128)} %reshape.523, f32[128]{0:T(128)S(1)} %get-tuple-element.27, f32[128]{0:T(128)S(1)} %get-tuple-element.25, f32[128]{0:T(128)S(1)} %get-tuple-element.24, s32[128]{0:T(128)S(1)} %get-tuple-element.26), kind=kOutput, calls=%fused_computation.20 | convolution fusion | flops 906051584 | bytes 4720640 | tf_op jit(solution)/shard_map/nzq,zw->qnw/dot_general | solution.py:88
  54.1 1.2 fusion.54
  55.2 1.4 %copy.32 = f32[1,24,1536]{2,1,0:T(8,128)S(1)} copy(f32[1,24,1536]{1,2,0:T(8,128)} %bitcast.27) | data formatting | bytes 294912 | tf_op jit(solution)/shard_map/slice | solution.py:21
  56.6 2.1 %collective-permute-start.1 = (f32[1,24,1536]{2,1,0:T(8,128)S(1)}, f32[1,24,1536]{2,1,0:T(8,128)S(1)}, u32[]{:S(2)}, u32[]{:S(2)}) collective-permute-start(f32[1,24,1536]{2,1,0:T(8,128)S(1)} %copy.32), channel_id=1, source_target_pairs={{0,16},{16,32},{32,48},{48,64},{64,80},{80,96},{96,112},{1,17},{17... | collective-permute-start | bytes 442376 | tf_op jit(solution)/shard_map/ppermute | solution.py:24
  58.7 2.5 %copy.30 = f32[384,12,128]{2,1,0:T(8,128)} copy(f32[384,12,128]{0,2,1:T(8,128)S(1)} %convolution_bitcast_fusion) | data formatting | bytes 4718592 | tf_op jit(solution)/shard_map/nzq,zw->qnw/transpose | solution.py:88
  61.2 0.2 copy.31
  61.5 1.3 %collective-permute-start = (f32[1,24,1536]{2,1,0:T(8,128)S(1)}, f32[1,24,1536]{2,1,0:T(8,128)S(1)}, u32[]{:S(2)}, u32[]{:S(2)}) collective-permute-start(f32[1,24,1536]{2,1,0:T(8,128)S(1)} %copy.31), channel_id=1, source_target_pairs={{16,0},{32,16},{48,32},{64,48},{80,64},{96,80},{112,96},{17,1},{33... | collective-permute-start | bytes 442376 | tf_op jit(solution)/shard_map/ppermute | solution.py:26
  62.8 2.7 %reshape.524 = f32[16,24,1536]{2,1,0:T(8,128)S(1)} reshape(f32[384,12,128]{2,1,0:T(8,128)} %copy.30) | data formatting | bytes 4718592 | tf_op jit(solution)/shard_map/reshape | solution.py:90
  65.7 2.1 %collective-permute-done = f32[1,24,1536]{2,1,0:T(8,128)S(1)} collective-permute-done((f32[1,24,1536]{2,1,0:T(8,128)S(1)}, f32[1,24,1536]{2,1,0:T(8,128)S(1)}, u32[]{:S(2)}, u32[]{:S(2)}) %collective-permute-start) | collective-permute-done | bytes 147488 | tf_op jit(solution)/shard_map/ppermute | solution.py:26
  68.0 4.9 %collective-permute-start.3 = (f32[18,1,1536]{2,1,0:T(1,128)S(1)}, f32[18,1,1536]{2,1,0:T(1,128)S(1)}, u32[]{:S(2)}, u32[]{:S(2)}) collective-permute-start(f32[18,1,1536]{2,1,0:T(1,128)S(1)} %get-tuple-element.8), channel_id=1, source_target_pairs={{0,1},{1,2},{2,3},{3,4},{4,5},{5,6},{6,7},{7,8},{8,9},{9,10},{10,1... | collective-permute-start | bytes 331784 | tf_op jit(solution)/shard_map/ppermute | solution.py:24
  72.9 2.3 %collective-permute-start.2 = (f32[18,1,1536]{2,1,0:T(1,128)S(1)}, f32[18,1,1536]{2,1,0:T(1,128)S(1)}, u32[]{:S(2)}, u32[]{:S(2)}) collective-permute-start(f32[18,1,1536]{2,1,0:T(1,128)S(1)} %get-tuple-element.9), channel_id=1, source_target_pairs={{1,0},{2,1},{3,2},{4,3},{5,4},{6,5},{7,6},{8,7},{9,8},{10,9},{11,1... | collective-permute-start | bytes 331784 | tf_op jit(solution)/shard_map/ppermute | solution.py:26
  75.2 5.4 %collective-permute-done.2 = f32[18,1,1536]{2,1,0:T(1,128)S(1)} collective-permute-done((f32[18,1,1536]{2,1,0:T(1,128)S(1)}, f32[18,1,1536]{2,1,0:T(1,128)S(1)}, u32[]{:S(2)}, u32[]{:S(2)}) %collective-permute-start.2) | collective-permute-done | bytes 110624 | tf_op jit(solution)/shard_map/ppermute | solution.py:26
  80.6 1.8 %select_maximum_fusion = f32[18,26,1538]{2,1,0:T(8,128)S(1)} fusion(f32[18,1,1536]{2,1,0:T(1,128)S(1)} %collective-permute-done.2, f32[18,24,1536]{2,1,0:T(8,128)S(1)} %constant_dynamic-update-slice_fusion, f32[18,1,1536]{2,1,0:T(1,128)S(1)} %collective-permute-done.3), kind=kLoop, calls=%fused_computation.2 | loop fusion | flops 5758272 | bytes 5754528 | tf_op jit(solution)/shard_map/concatenate | solution.py:22
  82.5 4.4 %multiply_reduce_fusion = (f32[]{:T(128)}, f32[16,24,1536]{2,1,0:T(8,128)}) fusion(f32[16,24,1536]{2,1,0:T(8,128)S(1)} %copy-done.1, f32[18,26,1538]{2,1,0:T(8,128)S(1)} %select_maximum_fusion, f32[18,24,1536]{2,1,0:T(8,128)S(1)} %constant_dynamic-update-slice_fusion, f32[18,1,1536]{2,1,0:T(1,128)S(1)} %collective-permute-done.3, ...), kind=kLoop, calls=%fused_computation.19 | loop fusion | flops 8257535 | bytes 14966788 | tf_op jit(solution)/shard_map/reduce_sum | solution.py:97
  86.9 7.5 %psum.35 = f32[]{:T(128)} all-reduce(f32[]{:T(128)} %get-tuple-element.6), channel_id=1, replica_groups=mesh['px_0'=4,'px_1'=2,'py_0'=4,'py_1'=2,'py_2'=2] {'px_0'}, use_global_device_ids=true, to_apply=%region_1.2 | all-reduce | flops 1 | bytes 8 | tf_op jit(solution)/shard_map/psum | solution.py:34
  94.3 4.4 %psum.36 = f32[]{:T(128)} all-reduce(f32[]{:T(128)} %psum.35), channel_id=1, replica_groups=mesh['px_0'=4,'px_1'=2,'py_0'=4,'py_1'=2,'py_2'=2] {'px_1'}, use_global_device_ids=true, to_apply=%region_2.3 | all-reduce | flops 1 | bytes 8 | tf_op jit(solution)/shard_map/psum | solution.py:34
  98.7 8.2 %psum.37 = f32[]{:T(128)} all-reduce(f32[]{:T(128)} %psum.36), channel_id=1, replica_groups=mesh['px_0'=4,'px_1'=2,'py_0'=4,'py_1'=2,'py_2'=2] {'py_0'}, use_global_device_ids=true, to_apply=%region_3.4 | all-reduce | flops 1 | bytes 8 | tf_op jit(solution)/shard_map/psum | solution.py:34
  106.9 5.9 %psum.38 = f32[]{:T(128)} all-reduce(f32[]{:T(128)} %psum.37), channel_id=1, replica_groups=mesh['px_0'=4,'px_1'=2,'py_0'=4,'py_1'=2,'py_2'=2] {'py_1'}, use_global_device_ids=true, to_apply=%region_4.5 | all-reduce | flops 1 | bytes 8 | tf_op jit(solution)/shard_map/psum | solution.py:34
  112.8 7.8 %psum.39 = f32[]{:T(128)} all-reduce(f32[]{:T(128)} %psum.38), channel_id=1, replica_groups=mesh['px_0'=4,'px_1'=2,'py_0'=4,'py_1'=2,'py_2'=2] {'py_2'}, use_global_device_ids=true, to_apply=%region_5.6 | all-reduce | flops 1 | bytes 8 | tf_op jit(solution)/shard_map/psum | solution.py:34
  (21 shorter events, 0.8 us)
Async XLA Ops:
  6.7 36.3 %all-to-all-start = ((bf16[12,128,384]{2,0,1:T(8,128)(2,1)}), bf16[12,128,384]{2,0,1:T(8,128)(2,1)}, u32[]{:S(2)}, u32[]{:S(2)}) async-start(bf16[12,128,384]{2,0,1:T(8,128)(2,1)} %copy.27), calls=%async_computation | async-start | bytes 3145728 | tf_op jit(solution)/shard_map/all_to_all | solution.py:84
  56.6 8.9 %collective-permute-start.1 = (f32[1,24,1536]{2,1,0:T(8,128)S(1)}, f32[1,24,1536]{2,1,0:T(8,128)S(1)}, u32[]{:S(2)}, u32[]{:S(2)}) collective-permute-start(f32[1,24,1536]{2,1,0:T(8,128)S(1)} %copy.32), channel_id=1, source_target_pairs={{0,16},{16,32},{32,48},{48,64},{64,80},{80,96},{96,112},{1,17},{17... | collective-permute-start | bytes 442376 | tf_op jit(solution)/shard_map/ppermute | solution.py:24
  61.5 6.3 %collective-permute-start = (f32[1,24,1536]{2,1,0:T(8,128)S(1)}, f32[1,24,1536]{2,1,0:T(8,128)S(1)}, u32[]{:S(2)}, u32[]{:S(2)}) collective-permute-start(f32[1,24,1536]{2,1,0:T(8,128)S(1)} %copy.31), channel_id=1, source_target_pairs={{16,0},{32,16},{48,32},{64,48},{80,64},{96,80},{112,96},{17,1},{33... | collective-permute-start | bytes 442376 | tf_op jit(solution)/shard_map/ppermute | solution.py:26
  65.5 17.0 %copy-start = (f32[16,24,1536]{2,1,0:T(8,128)}, f32[16,24,1536]{2,1,0:T(8,128)S(1)}, u32[]{:S(2)}) copy-start(f32[16,24,1536]{2,1,0:T(8,128)S(1)} %reshape.524) | copy-start | bytes 7077892
  68.0 7.2 %collective-permute-start.3 = (f32[18,1,1536]{2,1,0:T(1,128)S(1)}, f32[18,1,1536]{2,1,0:T(1,128)S(1)}, u32[]{:S(2)}, u32[]{:S(2)}) collective-permute-start(f32[18,1,1536]{2,1,0:T(1,128)S(1)} %get-tuple-element.8), channel_id=1, source_target_pairs={{0,1},{1,2},{2,3},{3,4},{4,5},{5,6},{6,7},{7,8},{8,9},{9,10},{10,1... | collective-permute-start | bytes 331784 | tf_op jit(solution)/shard_map/ppermute | solution.py:24
  72.9 9.5 %copy-start.1 = (f32[16,24,1536]{2,1,0:T(8,128)S(1)}, f32[16,24,1536]{2,1,0:T(8,128)}, u32[]{:S(2)}) copy-start(f32[16,24,1536]{2,1,0:T(8,128)} %param.5) | copy-start | bytes 7077892
  72.9 7.7 %collective-permute-start.2 = (f32[18,1,1536]{2,1,0:T(1,128)S(1)}, f32[18,1,1536]{2,1,0:T(1,128)S(1)}, u32[]{:S(2)}, u32[]{:S(2)}) collective-permute-start(f32[18,1,1536]{2,1,0:T(1,128)S(1)} %get-tuple-element.9), channel_id=1, source_target_pairs={{1,0},{2,1},{3,2},{4,3},{5,4},{6,5},{7,6},{8,7},{9,8},{10,9},{11,1... | collective-permute-start | bytes 331784 | tf_op jit(solution)/shard_map/ppermute | solution.py:26
where the time goes:
time: 123 us; the launch traced here: 122 us
  blocking collectives  33.7 us (27%)
  waiting for transfers between devices  29 us (24%)
  starting transfers between devices  22.5 us (18%)
  local copies, waits for them, and re-layouts  16.3 us (13%)
  other arithmetic  9.6 us (8%)
  matrix products  8.67 us (7%)
  between operations  2.7 us (2%)
    psum x5, blocking collectives, one_axis_at_a_time(): return functools.reduce(lax.psum, axes, x)  33.7 us
    all_to_all x1, waiting for transfers between devices, shards(): lax.all_to_all(scaled, PX_PY, split_axis=1, concat_axis=1, tiled=True)  21.4 us
    all_to_all x1, starting transfers between devices, shards(): lax.all_to_all(scaled, PX_PY, split_axis=1, concat_axis=1, tiled=True)  11.9 us
    ppermute x2, waiting for transfers between devices, with_halo(): lax.ppermute(head, axis, [((i + 1) % count, i) for i in range(ends)])  7.54 us
    ppermute x2, starting transfers between devices, with_halo(): lax.ppermute(tail, axis, [(i, (i + 1) % count) for i in range(ends)])  7.02 us
    reduce_sum x1, other arithmetic, shards(): local_sum = jnp.sum(residual * residual)  4.39 us
    dot_general x1, matrix products, shards(): jnp.einsum('nzq,zw->qnw', stacked, depth_table, precision=lax.Precision.H...  4.01 us
    dot_general x1, matrix products, apply_plane(): jnp.einsum('zpc,cv->zpv', layers.astype(jnp.float32), table, precision=la...  3.99 us
  transfers between devices with their start and end apart: 5, of which 3 were waited for; matrix products, arithmetic and copies ran while one was open for 7% of the time, Pallas kernels for 0%

commit v1 on v0

v1 whole, which is shorter than its diff:
```python
import functools

import jax
import jax.numpy as jnp
import numpy as np
from jax import lax
from jax.experimental import pallas as pl
from jax.experimental.pallas import tpu as pltpu
from jax.sharding import PartitionSpec as P

CX = 16
CY = 24
CELLS = CX * CY
NZ = 1536
PEERS = 128
LAYERS = 12
ROWS = 16
F32 = jnp.float32
BF16 = jnp.bfloat16
MESH = pl.DeviceIdType.MESH


def basis():
    a = np.arange(4.0)[:, None]
    i = np.arange(4.0)[None, :]
    weight = np.where(a == 0, np.sqrt(0.25), np.sqrt(0.5))
    return weight * np.cos(np.pi * (2 * i + 1) * a / 8)


def halves(table):
    hi = table.astype(np.float32).astype(BF16)
    lo = (table - hi.astype(np.float64)).astype(np.float32).astype(BF16)
    return hi, lo


def block_table(width):
    b = basis()
    n = np.arange(width)
    return np.where(n[:, None] // 4 == n[None, :] // 4, b[n[:, None] % 4, n[None, :] % 4], 0.0)


def tables():
    b = basis()
    plane = np.kron(block_table(CX), block_table(CY))
    plane_hi, plane_lo = halves(plane.T)
    lane_of = np.zeros((3, 64), np.int64)
    cell_of = np.zeros(256, np.int64)
    part_of = np.full(256, -1)
    for k in range(3):
        for e in range(64):
            lane_of[k, e] = k * 48 + e if e < 48 else 144 + k * 16 + e - 48
        for e in range(24):
            cell_of[k * 48 + e] = e
            cell_of[k * 48 + 24 + e] = 15 * CY + e
        for x in range(16):
            cell_of[144 + k * 16 + x] = x * CY
            cell_of[192 + k * 16 + x] = x * CY + 23
        for first, size in ((k * 48, 48), (144 + k * 16, 16), (192 + k * 16, 16)):
            part_of[first : first + size] = k
    edge = np.where(part_of[None, :] >= 0, plane[:, cell_of], 0.0)
    edge_hi, edge_lo = halves(edge)
    keep = (np.arange(ROWS)[:, None] // 4 == part_of[None, :]).astype(np.float32)
    mix = np.zeros((256, 256))
    for p in range(16):
        q = p + 1 if p % 2 else p - 1
        for r in range(4):
            for z in range(LAYERS):
                mix[p * 8 + 4 + r, p * 16 + z] = b[z % 4, r]
                if 0 <= q < 16:
                    mix[128 + p * 8 + 4 + r, q * 16 + z] = b[z % 4, r]
    mix_hi, mix_lo = halves(mix)
    pick = np.zeros((192, CELLS))
    for k in range(3):
        for e in range(64):
            pick[k * 64 + e, lane_of[k, e]] = 1
            pick[k * 64 + e, 192 + lane_of[k, e]] = 1
    left = np.concatenate([plane_hi, plane_lo, pick.astype(BF16)], axis=0)
    depth = np.zeros((2, 256, 256))
    place = np.zeros((2, 768, 256))
    for odd in range(2):
        for s in range(16):
            base = 64 * odd + s * LAYERS
            for z in range(LAYERS):
                for o in range(z // 4 * 4, z // 4 * 4 + 4):
                    depth[odd, s * 16 + z, base + o] = b[z % 4, o % 4]
            for k in range(3):
                for r in range(4):
                    place[odd, k * 256 + s * 16 + 12 + r, base + k * 4 + r] = 1
    depth_hi, depth_lo = halves(depth)
    column = np.arange(CELLS)
    spread = (column[:, None] % 24 == (column[None, :] // CY // 4) * 6 + column[None, :] % CY // 4).astype(BF16)
    return (
        spread,
        np.stack([edge_hi, edge_lo]),
        keep,
        np.stack([mix_hi, mix_lo]),
        left,
        np.stack([depth_hi, depth_lo], axis=1),
        place.astype(BF16),
    )


def dot(a, b):
    return lax.dot_general(a, b, (((1,), (0,)), ((), ())), preferred_element_type=F32)


def dot_rows(a, b):
    return lax.dot_general(a, b, (((1,), (1,)), ((), ())), preferred_element_type=F32)


def two(x):
    hi = x.astype(BF16)
    return hi, (x - hi.astype(F32)).astype(BF16)


def position():
    i, j = lax.axis_index("px"), lax.axis_index("py")
    return (j // 2) % 2 * 2 + i % 2, i // 2, j // 4, j % 2


def device_at(x, y, z, c):
    return lax.rem(y, 4) * 2 + lax.rem(x, 2), lax.rem(z, 4) * 4 + lax.rem(x, 4) // 2 * 2 + lax.rem(c, 2)


def beside(dx, dy, dz, dc):
    x, y, z, c = position()
    return device_at(x + dx, y + dy, z + dz, c + dc)


def ident(pair):
    return {"px": pair[0], "py": pair[1]}


def kernel(
    coef_hbm, expo_hbm, right_hbm, spread_hbm, edge_hbm, keep_hbm, mix_hbm, left_hbm, depth_hbm, place_hbm,
    dec_ref, res_ref, rms_ref,
    coef, expo, right, spread, edge, keep, mix, left, depth, place,
    sbuf, rbuf, ebuf, dpad, ext, pair_out, pair_in, part, parts,
    load_sem, step_sem, send_sem, recv_sem, pair_send, pair_recv, sum_send, sum_recv,
):
    x, y, z, c = position()
    me = lax.axis_index("px") * 16 + lax.axis_index("py")
    loads = [
        pltpu.make_async_copy(src, dst, load_sem.at[n])
        for n, (src, dst) in enumerate(
            (
                (coef_hbm, coef), (expo_hbm, expo), (spread_hbm, spread), (edge_hbm, edge), (keep_hbm, keep),
                (mix_hbm, mix), (left_hbm, left), (depth_hbm, depth), (place_hbm, place), (right_hbm, right),
            )
        )
    ]
    for load in loads:
        load.start()

    entry = pltpu.get_barrier_semaphore()
    for n in range(1, 8):
        pl.semaphore_signal(entry, inc=1, device_id=ident(beside(n // 2, 0, 0, n % 2)), device_id_type=MESH)
    for n in range(1, 4):
        pl.semaphore_signal(entry, inc=1, device_id=ident(beside(0, n, 0, 0)), device_id_type=MESH)
        pl.semaphore_signal(entry, inc=1, device_id=ident(beside(0, 0, n, 0)), device_id_type=MESH)

    def clear(g, _):
        sbuf[pl.ds(g * 16, 16)] = jnp.zeros((16, ROWS, CELLS), BF16)
        return 0

    lax.fori_loop(0, 8, clear, 0)
    ebuf[0] = jnp.zeros((128, 256), F32)
    ebuf[9] = jnp.zeros((128, 256), F32)

    for load in loads[:3]:
        load.wait()

    row16 = lax.broadcasted_iota(jnp.int32, (ROWS, CELLS), 0)
    owner = lax.broadcasted_iota(jnp.int32, (ROWS, CELLS), 1) // 24

    def scale(g, _):
        base = pl.multiple_of(g * 384, 128)
        power = jnp.exp2(expo[:, pl.ds(base, 384)].astype(F32))
        rows = jnp.where(row16 < 4, power[0:1], jnp.where(row16 < 8, power[1:2], power[2:3]))
        apart = jnp.concatenate([jnp.where(owner == j, rows, 0.0) for j in range(16)], axis=0).astype(BF16)
        factor = dot(apart, spread[...])
        for j in range(16):
            at = pl.multiple_of(g * (16 * CELLS) + j * CELLS, 128)
            held = coef[:, pl.ds(at, CELLS)].astype(F32)
            sbuf[g * 16 + j, 0:LAYERS, :] = (held * factor[j * 16 : j * 16 + LAYERS]).astype(BF16)
        return 0

    lax.fori_loop(0, 8, scale, 0)

    pl.semaphore_wait(entry, 13)
    for n in range(1, 4):
        pl.semaphore_signal(step_sem.at[0], inc=1, device_id=ident(beside(0, n, 0, 0)), device_id_type=MESH)

    for load in loads[3:6]:
        load.wait()
    lane = lax.broadcasted_iota(jnp.int32, (128, 256), 1)
    even = lax.broadcasted_iota(jnp.int32, (128, 256), 0) // 8 % 2 == 0

    def edges(g, _):
        held = sbuf[pl.ds(g * 16, 16)].reshape(256, CELLS)
        wide = dot(held, edge[0]) + dot(held, edge[1])
        wide = (wide.reshape(16, ROWS, 256) * keep[...][None]).reshape(256, 256)
        hi, lo = two(wide)
        mixed = dot(mix[0], hi) + dot(mix[1], hi) + dot(mix[0], lo)
        both = jnp.where(lane < 144, mixed[:128], mixed[128:])
        ebuf[g + 1] = jnp.where(even & (lane >= 144), pltpu.roll(both, 256 - 48, 1), both)
        return 0

    lax.fori_loop(0, 8, edges, 0)

    pl.semaphore_wait(step_sem.at[0], 3)
    for n in range(1, 4):
        pl.semaphore_signal(step_sem.at[1], inc=1, device_id=ident(beside(0, 0, n, 0)), device_id_type=MESH)

    low = lane % 48 < 24
    half = lax.broadcasted_iota(jnp.int32, (128, 128), 1) < 64

    def gather(g, _):
        value = jnp.where(lane < 144, jnp.where(low, ebuf[g + 2], ebuf[g]), ebuf[g + 1])
        hi = value.astype(BF16).astype(F32)
        lo = value - hi
        first = pltpu.roll(lo[:, :128], 64, 1)
        second = pltpu.roll(lo[:, 128:], 64, 1)
        line = jnp.concatenate(
            [hi[:, :128], jnp.where(half, hi[:, 128:], first), jnp.where(half, first, second)], axis=1
        ).reshape(16, 8, CELLS)
        tall = jnp.concatenate([jnp.zeros((16, 8, CELLS), F32), line], axis=1).astype(BF16)
        sbuf[pl.ds(g * 16, 16)] = sbuf[pl.ds(g * 16, 16)] + tall
        return 0

    lax.fori_loop(0, 8, gather, 0)
    rbuf[me] = sbuf[me]
    pl.semaphore_wait(step_sem.at[1], 3)

    def message(phase, n):
        m = n * 37 % 64
        there = beside(m // 2 % 4, m // 32 * 2 + phase, m // 8 % 4, m % 2)
        return pltpu.make_async_remote_copy(
            sbuf.at[there[0] * 16 + there[1]], rbuf.at[me], send_sem, recv_sem.at[phase],
            device_id=ident(there), device_id_type=MESH,
        )

    def start(phase):
        def one(n, _):
            message(phase, n).start()
            return 0

        lax.fori_loop(1 - phase, 64, one, 0)

    start(0)
    start(1)

    for load in loads[6:]:
        load.wait()

    here = ident(beside(0, 0, 0, 1))

    def pair_copy(n, at):
        return pltpu.make_async_remote_copy(
            pair_out.at[:, pl.ds(at, 384)], pair_in.at[:, pl.ds(at, 384)], pair_send.at[n], pair_recv.at[n],
            device_id=here, device_id_type=MESH,
        )

    def decode(phase, k):
        layer = lax.rem(y + phase + 2 * k, 4)
        at = pl.multiple_of(layer * 384, 128)
        cells, sides = [], []
        for odd in range(2):
            held = rbuf[pl.ds(layer * 32 + odd * 16, 16)].reshape(256, CELLS)
            wide = dot_rows(left[...], held)
            hi, lo = two(wide[:384] + wide[384:768])
            cells.append(dot(hi, depth[odd, 0]) + dot(lo, depth[odd, 0]) + dot(hi, depth[odd, 1]))
            hi, lo = two(jnp.concatenate([wide[768:832], wide[832:896], wide[896:960]], axis=1))
            sides.append(dot(hi, place[odd]) + dot(lo, place[odd]))

        def join(pieces):
            a, b = pieces
            return jnp.concatenate([a[:, :128], a[:, 128:] + b[:, :128], b[:, 128:]], axis=1)

        field, side = join(cells), join(sides)
        dec_ref[:, pl.ds(at, 384)] = field
        dpad[24:408, pl.ds(at, 384)] = field
        dpad[0:24, pl.ds(at, 384)] = side[24:48]
        dpad[408:432, pl.ds(at, 384)] = side[0:24]
        ext[:, pl.ds(at, 384)] = side[48:64]
        cube = field.reshape(CX, CY, 384)
        pair_out[:, pl.ds(at, 384)] = jnp.where(c == 0, cube[:, 23, :], cube[:, 0, :])
        return at

    for phase in range(2):
        count = 63 + phase
        pltpu.make_async_copy(rbuf.at[pl.ds(0, count)], rbuf.at[pl.ds(0, count)], recv_sem.at[phase]).wait()
        places = [decode(phase, k) for k in range(2)]
        for k in range(2):
            pair_copy(phase * 2 + k, places[k]).start()
    for phase in range(2):
        for k in range(2):
            pair_copy(phase * 2 + k, pl.multiple_of(lax.rem(y + phase + 2 * k, 4) * 384, 128)).wait()

    column = lax.broadcasted_iota(jnp.int32, (CY, NZ), 1)
    row = lax.broadcasted_iota(jnp.int32, (CY, NZ), 0)

    def slab(n, total):
        at = pl.multiple_of(n * CY, 8)
        own = dpad[pl.ds(at + CY, CY), :]
        near = dpad[pl.ds(at, CY), :] + dpad[pl.ds(at + 2 * CY, CY), :]
        inner, outer = pair_in[pl.ds(n, 1), :], ext[pl.ds(n, 1), :]
        below = jnp.where(c == 0, outer, inner)
        above = jnp.where(c == 0, inner, outer)
        near = near + jnp.where(row == 0, below, pltpu.roll(own, 1, 0))
        near = near + jnp.where(row == CY - 1, above, pltpu.roll(own, CY - 1, 0))
        near = near + jnp.where(column == 0, 0.0, pltpu.roll(own, 1, 1))
        near = near + jnp.where(column == NZ - 1, 0.0, pltpu.roll(own, NZ - 1, 1))
        value = right[pl.ds(at, CY), :] - (6.0 * own - near)
        res_ref[pl.ds(at, CY), :] = value
        square = value * value
        square = square[0:8] + square[8:16] + square[16:24]
        return total + sum(square[:, k * 128 : (k + 1) * 128] for k in range(NZ // 128))

    total = lax.fori_loop(0, CX, slab, jnp.zeros((8, 128), F32))
    part[...] = jnp.sum(total, axis=0, keepdims=True)
    parts[me] = part[...]

    def note(n):
        m = PEERS - n
        there = beside(m // 2 % 4, m // 8 % 4, m // 32, m % 2)
        return pltpu.make_async_remote_copy(
            part, parts.at[me], sum_send, sum_recv, device_id=ident(there), device_id_type=MESH
        )

    def tell(n, _):
        note(n).start()
        return 0

    lax.fori_loop(1, PEERS, tell, 0)
    everyone = pl.ds(0, PEERS - 1)
    pltpu.make_async_copy(sbuf.at[everyone], sbuf.at[everyone], send_sem).wait()
    pltpu.make_async_copy(parts.at[everyone], parts.at[everyone], sum_send).wait()
    pltpu.make_async_copy(parts.at[everyone], parts.at[everyone], sum_recv).wait()
    whole = jnp.sum(jnp.sum(parts[...], axis=0), axis=1, keepdims=True)
    rms_ref[...] = jnp.broadcast_to(jnp.sqrt(whole / (PEERS * CELLS * NZ) + 1e-06), (8, 128))


def shards(coefficients, exponents, right_side):
    constants = tables()
    any_space = pl.BlockSpec(memory_space=pl.ANY)
    vmem = pl.BlockSpec(memory_space=pltpu.VMEM)
    right = right_side.reshape(CELLS, NZ)
    operands = (coefficients, exponents, right, *constants)
    held = [pltpu.VMEM(o.shape, o.dtype) for o in operands]
    sem = pltpu.SemaphoreType
    field = jax.ShapeDtypeStruct((CELLS, NZ), F32)
    decoded, residual, rms = pl.pallas_call(
        kernel,
        name="exchange",
        out_shape=(field, field, jax.ShapeDtypeStruct((8, 128), F32)),
        in_specs=[any_space] * len(operands),
        out_specs=(vmem, vmem, vmem),
        scratch_shapes=[
            *held,
            pltpu.VMEM((PEERS, ROWS, CELLS), BF16),
            pltpu.VMEM((PEERS, ROWS, CELLS), BF16),
            pltpu.VMEM((10, 128, 256), F32),
            pltpu.VMEM((CELLS + 2 * CY, NZ), F32),
            pltpu.VMEM((CX, NZ), F32),
            pltpu.VMEM((CX, NZ), F32),
            pltpu.VMEM((CX, NZ), F32),
            pltpu.VMEM((1, 128), F32),
            pltpu.VMEM((PEERS, 1, 128), F32),
            sem.DMA((len(operands),)),
            sem.REGULAR((2,)),
            sem.DMA,
            sem.DMA((2,)),
            sem.DMA((4,)),
            sem.DMA((4,)),
            sem.DMA,
            sem.DMA,
        ],
        compiler_params=pltpu.CompilerParams(collective_id=0, has_side_effects=True, vmem_limit_bytes=60 << 20),
    )(*operands)
    shape = (CX, CY, NZ)
    return decoded.reshape(shape), residual.reshape(shape), rms[0, 0]


def solution(mesh):
    placed = (P(("px", "py"), None), P(("px", "py"), None), P("px", "py", None))
    return jax.shard_map(
        shards,
        mesh=mesh,
        in_specs=placed,
        out_specs=(P("px", "py", None), P("px", "py", None), P()),
        check_vma=False,
    )
```

time: 123 us -> 62.1 us (0.50)
  Pallas kernels: 0 us -> 55.3 us
  blocking collectives: 33.7 us -> 0 us
  waiting for transfers between devices: 29 us -> 0 us
  starting transfers between devices: 22.5 us -> 0 us
  local copies, waits for them, and re-layouts: 16.3 us -> 5.97 us
  other arithmetic: 9.6 us -> 0 us
  matrix products: 8.67 us -> 0 us
  between operations: 2.7 us -> 0.64 us
    pallas_call x0 -> x1, Pallas kernels: none -> 55.3 us  [shards(): pl.pallas_call(kernel, name='exchange', out_shape=(field, field, jax.Shap...]
    psum x5 -> x0, blocking collectives: 33.7 us -> none  [one_axis_at_a_time(): return functools.reduce(lax.psum, axes, x)]
    all_to_all x1 -> x0, waiting for transfers between devices: 21.4 us -> none  [shards(): lax.all_to_all(scaled, PX_PY, split_axis=1, concat_axis=1, tiled=True)]
    all_to_all x1 -> x0, starting transfers between devices: 11.9 us -> none  [shards(): lax.all_to_all(scaled, PX_PY, split_axis=1, concat_axis=1, tiled=True)]
    ppermute x4 -> x0, starting transfers between devices: 10.6 us -> none  [the longest x2 7.02 us: with_halo(): lax.ppermute(tail, axis, [(i, (i + 1) % count) for i in range(ends)])]
    dot_general x3 -> x0, matrix products: 8.67 us -> none  [the longest x1 4.01 us: shards(): jnp.einsum('nzq,zw->qnw', stacked, depth_table, precision=lax.Precision.H...]
    ppermute x4 -> x0, waiting for transfers between devices: 7.55 us -> none  [the longest x2 7.54 us: with_halo(): lax.ppermute(head, axis, [((i + 1) % count, i) for i in range(ends)])]
    reshape x4 -> x0, local copies, waits for them, and re-layouts: 6.73 us -> none  [the longest x1 2.69 us: shards(): decoded = jnp.einsum('nzq,zw->qnw', stacked, depth_table, precision=lax.P...]
  transfers between devices with their start and end apart: 5 -> 0, of which waited for: 3 -> 0; matrix products, arithmetic and copies ran while one was open for 7% -> 0% of each run, Pallas kernels for 0% -> 0%
where the time goes in v1:
time: 62.1 us; the launch traced here: 61.9 us
  Pallas kernels  55.3 us (89%)
  local copies, waits for them, and re-layouts  5.97 us (10%)
  between operations  0.64 us (1%)
    pallas_call x1, Pallas kernels, shards(): pl.pallas_call(kernel, name='exchange', out_shape=(field, field, jax.Shap...  55.3 us
    unnamed x4, local copies, waits for them, and re-layouts  4.79 us

profile of v1, /device:TPU:1, one launch (start us, length us, event | category | flops | bytes accessed | tf_op | source)
XLA Modules:
  0.0 61.9 jit_solution(8195613973702969632)
XLA Ops:
  0.6 55.3 %exchange.1 = (f32[384,1536]{1,0:T(8,128)}, f32[384,1536]{1,0:T(8,128)}, f32[8,128]{1,0:T(8,128)}) custom-call(bf16[12,49152]{1,0:T(8,128)(2,1)} %coef_hbm.1, s32[3,3072]{1,0:T(4,128)} %expo_hbm.1, f32[384,1536]{1,0:T(8,128)} %bitcast.4, bf16[384,384]{1,0:T(8,128)(2,1)} %constant.14.clone.spread_hbm, bf16[2,384,256]{2,1,0:T(8,128)(2,1)} %constant.15.clone.edge_hbm, ...), custom_call_target="tpu_custom_call" | custom-call | tf_op jit(solution)/shard_map/exchange/pallas_call | solution.py:353
  56.0 1.2 %slice.3 = f32[1,1]{1,0:T(1,128)} slice(f32[8,128]{1,0:T(8,128)} %get-tuple-element.8), slice={[0:1], [0:1]} | slice | bytes 8 | tf_op jit(solution)/shard_map/slice | solution.py:382
  57.2 0.0 copy-start
  57.2 3.4 %copy.15 = f32[16,24,1536]{2,1,0:T(8,128)} copy(f32[16,24,1536]{2,1,0:T(8,128)} %bitcast.6) | data formatting | bytes 4718592
  60.5 0.0 copy-done
  60.5 1.4 %copy.16 = f32[16,24,1536]{2,1,0:T(8,128)} copy(f32[16,24,1536]{2,1,0:T(8,128)S(1)} %bitcast.5) | data formatting | bytes 4718592
Async XLA Ops:
  57.2 3.4 %copy-start = (f32[384,1536]{1,0:T(8,128)S(1)}, f32[384,1536]{1,0:T(8,128)}, u32[]{:S(2)}) copy-start(f32[384,1536]{1,0:T(8,128)} %get-tuple-element.7) | copy-start | bytes 7077892

commit v2 on v1

v2 whole, which is shorter than its diff:
```python
import functools

import jax
import jax.numpy as jnp
import numpy as np
from jax import lax
from jax.experimental import pallas as pl
from jax.experimental.pallas import tpu as pltpu
from jax.sharding import PartitionSpec as P

CX = 16
CY = 24
CELLS = CX * CY
NZ = 1536
PEERS = 128
LAYERS = 12
ROWS = 16
F32 = jnp.float32
BF16 = jnp.bfloat16
MESH = pl.DeviceIdType.MESH
UNROLL = 2
VMEM_BYTES = 40 << 20


def basis():
    a = np.arange(4.0)[:, None]
    i = np.arange(4.0)[None, :]
    weight = np.where(a == 0, np.sqrt(0.25), np.sqrt(0.5))
    return weight * np.cos(np.pi * (2 * i + 1) * a / 8)


def halves(table):
    hi = table.astype(np.float32).astype(BF16)
    lo = (table - hi.astype(np.float64)).astype(np.float32).astype(BF16)
    return hi, lo


def block_table(width):
    b = basis()
    n = np.arange(width)
    return np.where(n[:, None] // 4 == n[None, :] // 4, b[n[:, None] % 4, n[None, :] % 4], 0.0)


def tables():
    b = basis()
    plane = np.kron(block_table(CX), block_table(CY))
    plane_hi, plane_lo = halves(plane.T)
    lane_of = np.zeros((3, 64), np.int64)
    cell_of = np.zeros(256, np.int64)
    part_of = np.full(256, -1)
    for k in range(3):
        for e in range(64):
            lane_of[k, e] = k * 48 + e if e < 48 else 144 + k * 16 + e - 48
        for e in range(24):
            cell_of[k * 48 + e] = e
            cell_of[k * 48 + 24 + e] = 15 * CY + e
        for x in range(16):
            cell_of[144 + k * 16 + x] = x * CY
            cell_of[192 + k * 16 + x] = x * CY + 23
        for first, size in ((k * 48, 48), (144 + k * 16, 16), (192 + k * 16, 16)):
            part_of[first : first + size] = k
    edge = np.where(part_of[None, :] >= 0, plane[:, cell_of], 0.0)
    edge_hi, edge_lo = halves(edge)
    part = np.broadcast_to(part_of[None, :], (8, 256)).astype(np.int32)
    turn = np.zeros((4, 8, 128), np.float32)
    for s in range(4):
        for r in range(4, 8):
            turn[s, r, :] = b[(r + s) % 4, r % 4]
    pick = np.zeros((192, 256))
    for k in range(3):
        for e in range(64):
            pick[k * 64 + e, lane_of[k, e]] = 1
    pick_hi = pick.astype(BF16)
    pick_lo = np.roll(pick, 64, axis=1).astype(BF16)
    left = np.stack(
        [
            np.concatenate([plane_hi[:192, :256], plane_lo[:192, :256], pick_hi]),
            np.concatenate([plane_hi[192:, 128:], plane_lo[192:, 128:], pick_lo]),
        ]
    )
    depth = np.zeros((2, 256, 256))
    place = np.zeros((2, 768, 256))
    for odd in range(2):
        for s in range(16):
            base = 64 * odd + s * LAYERS
            for z in range(LAYERS):
                for o in range(z // 4 * 4, z // 4 * 4 + 4):
                    depth[odd, s * 16 + z, base + o] = b[z % 4, o % 4]
            for k in range(3):
                for r in range(4):
                    place[odd, k * 256 + s * 16 + 12 + r, base + k * 4 + r] = 1
    depth_hi, depth_lo = halves(depth)
    column = np.arange(CELLS)
    spread = (column[:, None] % 24 == (column[None, :] // CY // 4) * 6 + column[None, :] % CY // 4).astype(BF16)
    return (
        spread,
        np.concatenate([edge_hi, edge_lo], axis=1),
        part,
        turn,
        left,
        np.stack([depth_hi, depth_lo], axis=1),
        place.astype(BF16),
    )


def dot(a, b):
    return lax.dot_general(a, b, (((1,), (0,)), ((), ())), preferred_element_type=F32)


def dot_rows(a, b):
    return lax.dot_general(a, b, (((1,), (1,)), ((), ())), preferred_element_type=F32)


def two(x):
    hi = x.astype(BF16)
    return hi, (x - hi.astype(F32)).astype(BF16)


def position():
    i, j = lax.axis_index("px"), lax.axis_index("py")
    return ((j >> 1) & 1) * 2 + (i & 1), i >> 1, j >> 2, j & 1


class Peers:
    def __init__(self):
        x, y, z, c = position()
        xs = [(x + d) & 3 for d in range(4)]
        self.x_low = [v & 1 for v in xs]
        self.x_high = [v & 2 for v in xs]
        self.y_part = [((y + d) & 3) * 2 for d in range(4)]
        self.z = z
        self.y = y
        self.core = [c, 1 - c]

    def z_part(self, d):
        return ((self.z + d) & 3) * 4

    def at(self, dx, dy, dz, dc):
        y = self.y_part[dy] if isinstance(dy, int) else ((self.y + dy) & 3) * 2
        return y + self.x_low[dx], self.z_part(dz) + self.x_high[dx] + self.core[dc]


def ident(pair):
    return {"px": pair[0], "py": pair[1]}


def kernel(
    coef_hbm, expo_hbm, right_hbm, spread_hbm, edge_hbm, part_hbm, turn_hbm, left_hbm, depth_hbm, place_hbm,
    dec_ref, res_ref, rms_ref,
    coef, expo, right, spread, edge, part_of, turn, left, depth, place,
    sbuf, rbuf, ebuf, dpad, ext, pair_out, pair_in, part, parts,
    load_sem, step_sem, send_sem, recv_sem, pair_send, pair_recv, sum_send, sum_recv,
):
    x, y, z, c = position()
    peers = Peers()
    me = lax.axis_index("px") * 16 + lax.axis_index("py")
    loads = [
        pltpu.make_async_copy(src, dst, load_sem.at[n])
        for n, (src, dst) in enumerate(
            (
                (coef_hbm, coef), (expo_hbm, expo), (spread_hbm, spread), (edge_hbm, edge), (part_hbm, part_of),
                (turn_hbm, turn), (left_hbm, left), (depth_hbm, depth), (place_hbm, place), (right_hbm, right),
            )
        )
    ]
    for load in loads:
        load.start()

    entry = pltpu.get_barrier_semaphore()
    for n in range(1, 8):
        pl.semaphore_signal(entry, inc=1, device_id=ident(peers.at(n // 2, 0, 0, n % 2)), device_id_type=MESH)
    for n in range(1, 4):
        pl.semaphore_signal(entry, inc=1, device_id=ident(peers.at(0, n, 0, 0)), device_id_type=MESH)
        pl.semaphore_signal(entry, inc=1, device_id=ident(peers.at(0, 0, n, 0)), device_id_type=MESH)

    def clear(g, _):
        sbuf[pl.ds(g * 16, 16), 8:16, :] = jnp.zeros((16, 8, CELLS), BF16)
        ebuf[g + 1, 0] = jnp.zeros((8, 256), F32)
        ebuf[g + 1, 17] = jnp.zeros((8, 256), F32)
        return 0

    lax.fori_loop(0, 8, clear, 0)
    ebuf[0] = jnp.zeros((18, 8, 256), F32)
    ebuf[9] = jnp.zeros((18, 8, 256), F32)

    with jax.named_scope("s_load"):
        for load in loads[:6]:
            load.wait()

    row16 = lax.broadcasted_iota(jnp.int32, (ROWS, CELLS), 0)
    owner = lax.broadcasted_iota(jnp.int32, (ROWS, CELLS), 1) // 24
    upper = lax.broadcasted_iota(jnp.int32, (16, 8, 256), 1) < 4

    def scale(g, _):
        base = pl.multiple_of(g * 384, 128)
        power = jnp.exp2(expo[:, pl.ds(base, 384)].astype(F32))
        rows = jnp.where(row16 < 4, power[0:1], jnp.where(row16 < 8, power[1:2], power[2:3]))
        apart = jnp.concatenate([jnp.where(owner == j, rows, 0.0) for j in range(16)], axis=0).astype(BF16)
        factor = dot(apart, spread[...])
        for j in range(16):
            at = pl.multiple_of(g * (16 * CELLS) + j * CELLS, 128)
            held = coef[:, pl.ds(at, CELLS)].astype(F32)
            sbuf[g * 16 + j, 0:LAYERS, :] = (held * factor[j * 16 : j * 16 + LAYERS]).astype(BF16)
        return 0

    def edges(g, _):
        held = sbuf[pl.ds(g * 16, 16)].reshape(256, CELLS)
        wide = dot(held, edge[...])
        wide = (wide[:, :256] + wide[:, 256:]).reshape(16, ROWS, 256)
        first, second = wide[:, :8], wide[:, 8:]
        first_turned, second_turned = pltpu.roll(first, 4, 1), pltpu.roll(second, 4, 1)
        kind = part_of[...][None]
        four = jnp.where(
            kind == 0,
            jnp.where(upper, first, first_turned),
            jnp.where(
                kind == 1, jnp.where(upper, first_turned, first), jnp.where(upper, second, second_turned)
            ),
        )
        weights = [jnp.concatenate([turn[s], turn[s]], axis=1)[None] for s in range(4)]
        mixed = four * weights[0]
        for s in range(1, 4):
            mixed = mixed + pltpu.roll(four, 8 - s, 1) * weights[s]
        ebuf[g + 1, 1:17] = mixed
        return 0

    with jax.named_scope("s_scale"):
        lax.fori_loop(0, 8, scale, 0, unroll=UNROLL)

    with jax.named_scope("s_bar1"):
        pl.semaphore_wait(entry, 13)
    for n in range(1, 4):
        pl.semaphore_signal(step_sem.at[0], inc=1, device_id=ident(peers.at(0, n, 0, 0)), device_id_type=MESH)

    with jax.named_scope("s_edges"):
        lax.fori_loop(0, 8, edges, 0, unroll=UNROLL)

    with jax.named_scope("s_bar2"):
        pl.semaphore_wait(step_sem.at[0], 3)
    for n in range(1, 4):
        pl.semaphore_signal(step_sem.at[1], inc=1, device_id=ident(peers.at(0, 0, n, 0)), device_id_type=MESH)

    lane = lax.broadcasted_iota(jnp.int32, (16, 8, 256), 2)
    low = lane % 48 < 24
    across = lane < 144
    half = lax.broadcasted_iota(jnp.int32, (16, 8, 128), 2) < 64
    even = lax.broadcasted_iota(jnp.int32, (16, 8, 128), 0) % 2 == 0

    def gather(g, _):
        value = jnp.where(low, ebuf[g + 2, 1:17], ebuf[g, 1:17])
        along = jnp.where(even, pltpu.roll(ebuf[g + 1, 0:16, :, 128:], 80, 2), ebuf[g + 1, 2:18, :, 128:])
        one = value[:, :, :128]
        two_ = jnp.where(across[:, :, 128:], value[:, :, 128:], along)
        one_hi = one.astype(BF16).astype(F32)
        two_hi = two_.astype(BF16).astype(F32)
        first = pltpu.roll(one - one_hi, 64, 2)
        second = pltpu.roll(two_ - two_hi, 64, 2)
        line = jnp.concatenate([one_hi, jnp.where(half, two_hi, first), jnp.where(half, first, second)], axis=2)
        tall = jnp.concatenate([jnp.zeros((16, 8, CELLS), F32), line], axis=1).astype(BF16)
        sbuf[pl.ds(g * 16, 16)] = sbuf[pl.ds(g * 16, 16)] + tall
        return 0

    with jax.named_scope("s_gather"):
        lax.fori_loop(0, 8, gather, 0)
    rbuf[me] = sbuf[me]
    with jax.named_scope("s_bar3"):
        pl.semaphore_wait(step_sem.at[1], 3)

    def start(phase):
        def one(i, _):
            for j in range(8):
                def go(j=j):
                    there = peers.at((j & 1) * 2 + phase % 2, (j >> 1 & 1) * 2 + phase // 2, i + j, j >> 2)
                    pltpu.make_async_remote_copy(
                        sbuf.at[there[0] * 16 + there[1]], rbuf.at[me], send_sem, recv_sem.at[phase],
                        device_id=ident(there), device_id_type=MESH,
                    ).start()

                if phase == 0 and j == 0:
                    pl.when(i > 0)(go)
                else:
                    go()
            return 0

        lax.fori_loop(0, 4, one, 0)

    with jax.named_scope("s_start"):
        for phase in range(4):
            start(phase)

    for load in loads[6:]:
        load.wait()

    def wipe(n, _):
        dpad[n] = jnp.zeros((CY, NZ + 256), F32)
        return 0

    lax.fori_loop(0, CX + 2, wipe, 0)
    ext[...] = jnp.zeros((CX, NZ), F32)

    here = ident(peers.at(0, 0, 0, 1))

    def layer(parity, k):
        return (y + parity + 2 * k) & 3

    def pair_copy(parity, k):
        at = pl.multiple_of(layer(parity, k) * 384, 128)
        n = parity * 2 + k
        return pltpu.make_async_remote_copy(
            pair_out.at[:, pl.ds(at, 384)], pair_in.at[:, pl.ds(at, 384)], pair_send.at[n], pair_recv.at[n],
            device_id=here, device_id_type=MESH,
        )

    def pair_start(parity, k):
        at = layer(parity, k) * 384
        lanes = pl.ds(pl.multiple_of(at + 128, 128), 384)
        last = dpad[1 : CX + 1, CY - 8 :, lanes][:, 7, :]
        first = dpad[1 : CX + 1, 0:8, lanes][:, 0, :]
        pair_out[:, pl.ds(pl.multiple_of(at, 128), 384)] = jnp.where(c == 0, last, first)
        pair_copy(parity, k).start()

    def decode(phase, k):
        odd = (x + phase) & 1
        group = layer(phase // 2, k) * 2 + odd
        at = layer(phase // 2, k) * 384 + odd * 128
        held = rbuf[pl.ds(group * 16, 16)].reshape(256, CELLS)
        near = dot_rows(left[0], held[:, :256])
        far = dot_rows(left[1], held[:, 128:])
        hi, lo = two(jnp.concatenate([near[:192] + near[192:384], far[:192] + far[192:384]], axis=0))
        table = depth[odd, 0]
        field = dot(hi, table) + dot(lo, table) + dot(hi, depth[odd, 1])
        side_hi = jnp.concatenate([near[384:448], near[448:512], near[512:576]], axis=1).astype(BF16)
        side_lo = jnp.concatenate([far[384:448], far[448:512], far[512:576]], axis=1).astype(BF16)
        table = place[odd]
        side = dot(side_hi, table) + dot(side_lo, table)
        lanes = pl.ds(pl.multiple_of(at + 128, 128), 256)
        dpad[1 : CX + 1, :, lanes] += field.reshape(CX, CY, 256)
        dpad[0, :, lanes] += side[24:48]
        dpad[CX + 1, :, lanes] += side[0:24]
        ext[:, pl.ds(pl.multiple_of(at, 128), 256)] += side[48:64]

    column = lax.broadcasted_iota(jnp.int32, (CY, 384), 1)
    row = lax.broadcasted_iota(jnp.int32, (CY, 384), 0)
    tile = lax.broadcasted_iota(jnp.int32, (CY, 128), 1)

    def squares(value):
        value = value * value
        value = value[0:8] + value[8:16] + value[16:24]
        return sum(value[:, k * 128 : (k + 1) * 128] for k in range(value.shape[1] // 128))

    def residual(parity, k, total):
        at = layer(parity, k) * 384
        lanes = pl.ds(pl.multiple_of(at, 128), 384)
        inside = pl.ds(pl.multiple_of(at + 128, 128), 384)

        def slab(n, total):
            rows = pl.multiple_of(n * CY, 8)
            own = dpad[n + 1, :, inside]
            near = dpad[n, :, inside] + dpad[n + 2, :, inside]
            inner, outer = pair_in[pl.ds(n, 1), lanes], ext[pl.ds(n, 1), lanes]
            below = jnp.where(c == 0, outer, inner)
            above = jnp.where(c == 0, inner, outer)
            near = near + jnp.where(row == 0, below, pltpu.roll(own, 1, 0))
            near = near + jnp.where(row == CY - 1, above, pltpu.roll(own, CY - 1, 0))
            back, forth = pltpu.roll(own, 1, 1), pltpu.roll(own, 383, 1)
            if parity == 0:
                back = jnp.where(column == 0, 0.0, back)
                forth = jnp.where(column == 383, 0.0, forth)
            else:
                prior = dpad[n + 1, :, pl.ds(pl.multiple_of(at, 128), 128)]
                later = dpad[n + 1, :, pl.ds(pl.multiple_of(at + 512, 128), 128)]
                back = jnp.concatenate(
                    [jnp.where(tile == 0, pltpu.roll(prior, 1, 1), back[:, :128]), back[:, 128:]], axis=1
                )
                forth = jnp.concatenate(
                    [forth[:, :256], jnp.where(tile == 127, pltpu.roll(later, 127, 1), forth[:, 256:])], axis=1
                )
            value = right[pl.ds(rows, CY), lanes] - (6.0 * own - (near + back + forth))
            dec_ref[pl.ds(rows, CY), lanes] = own
            res_ref[pl.ds(rows, CY), lanes] = value
            if parity == 0:
                value = jnp.where((column > 0) & (column < 383), value, 0.0)
            return total + squares(value)

        return lax.fori_loop(0, CX, slab, total, unroll=4)

    def seam(k, total):
        at = layer(0, k) * 384

        def slab(n, total):
            rows = pl.multiple_of(n * CY, 8)
            out = pl.ds(rows, CY)
            front = pl.ds(pl.multiple_of(at, 128), 128)
            prior = pltpu.roll(dpad[n + 1, :, front], 1, 1)
            value = res_ref[out, front] + jnp.where(tile == 0, prior, 0.0)
            res_ref[out, front] = value
            total = total + squares(jnp.where(tile == 0, value, 0.0))
            back = pl.ds(pl.multiple_of(at + 256, 128), 128)
            later = pltpu.roll(dpad[n + 1, :, pl.ds(pl.multiple_of(at + 512, 128), 128)], 127, 1)
            value = res_ref[out, back] + jnp.where(tile == 127, later, 0.0)
            res_ref[out, back] = value
            return total + squares(jnp.where(tile == 127, value, 0.0))

        return lax.fori_loop(0, CX, slab, total, unroll=4)

    total = jnp.zeros((8, 128), F32)
    for phase in range(4):
        count = 32 - (phase == 0)
        block = rbuf.at[pl.ds(0, count)]
        with jax.named_scope("s_wait"):
            pltpu.make_async_copy(block, block, recv_sem.at[phase]).wait()
        with jax.named_scope("s_decode"):
            for k in range(2):
                decode(phase, k)
                if phase % 2 == 1:
                    pair_start(phase // 2, k)
        if phase == 2:
            with jax.named_scope("s_early"):
                for k in range(2):
                    pair_copy(0, k).wait()
                    total = residual(0, k, total)
    with jax.named_scope("s_seam"):
        for k in range(2):
            total = seam(k, total)
    with jax.named_scope("s_pair"):
        for k in range(2):
            pair_copy(1, k).wait()
    with jax.named_scope("s_late"):
        for k in range(2):
            total = residual(1, k, total)

    part[...] = jnp.sum(total, axis=0, keepdims=True)
    parts[me] = part[...]

    def tell(i, _):
        for j in range(8):
            def go(j=j):
                there = peers.at((2, 1, 3, 0)[j >> 1], i + 2, (i >> 2) + 2, 1 - (j & 1))
                pltpu.make_async_remote_copy(
                    part, parts.at[me], sum_send, sum_recv, device_id=ident(there), device_id_type=MESH
                ).start()

            if j == 7:
                pl.when(i != 10)(go)
            else:
                go()
        return 0

    with jax.named_scope("s_tell"):
        lax.fori_loop(0, 16, tell, 0)
    everyone = pl.ds(0, PEERS - 1)
    with jax.named_scope("s_sent"):
        pltpu.make_async_copy(sbuf.at[everyone], sbuf.at[everyone], send_sem).wait()
    with jax.named_scope("s_sum"):
        pltpu.make_async_copy(parts.at[everyone], parts.at[everyone], sum_recv).wait()
    pltpu.make_async_copy(parts.at[everyone], parts.at[everyone], sum_send).wait()
    whole = jnp.sum(jnp.sum(parts[...], axis=0), axis=1, keepdims=True)
    rms_ref[0, 0] = jnp.sqrt(whole / (PEERS * CELLS * NZ) + 1e-06)[0, 0]


def deliver(dec_ref, res_ref, dec_out, res_out, sems):
    copies = [
        pltpu.make_async_copy(src, dst, sems.at[n])
        for n, (src, dst) in enumerate(((dec_ref, dec_out), (res_ref, res_out)))
    ]
    for copy in copies:
        copy.start()
    for copy in copies:
        copy.wait()


def shards(coefficients, exponents, right_side):
    constants = tables()
    any_space = pl.BlockSpec(memory_space=pltpu.HBM)
    vmem = pl.BlockSpec(memory_space=pltpu.VMEM)
    right = right_side.reshape(CELLS, NZ)
    operands = (coefficients, exponents, right, *constants)
    operands = tuple(pltpu.with_memory_space_constraint(jnp.asarray(o), pltpu.HBM) for o in operands)
    held = [pltpu.VMEM(o.shape, o.dtype) for o in operands]
    sem = pltpu.SemaphoreType
    field = jax.ShapeDtypeStruct((CELLS, NZ), F32)
    decoded, residual, rms = pl.pallas_call(
        kernel,
        name="exchange",
        out_shape=(field, field, jax.ShapeDtypeStruct((1, 1), F32)),
        in_specs=[any_space] * len(operands),
        out_specs=(vmem, vmem, pl.BlockSpec(memory_space=pltpu.SMEM)),
        scratch_shapes=[
            *held,
            pltpu.VMEM((PEERS, ROWS, CELLS), BF16),
            pltpu.VMEM((PEERS, ROWS, CELLS), BF16),
            pltpu.VMEM((10, 18, 8, 256), F32),
            pltpu.VMEM((CX + 2, CY, NZ + 256), F32),
            pltpu.VMEM((CX, NZ), F32),
            pltpu.VMEM((CX, NZ), F32),
            pltpu.VMEM((CX, NZ), F32),
            pltpu.VMEM((1, 128), F32),
            pltpu.VMEM((PEERS, 1, 128), F32),
            sem.DMA((len(operands),)),
            sem.REGULAR((2,)),
            sem.DMA,
            sem.DMA((4,)),
            sem.DMA((4,)),
            sem.DMA((4,)),
            sem.DMA,
            sem.DMA,
        ],
        compiler_params=pltpu.CompilerParams(collective_id=0, has_side_effects=True, vmem_limit_bytes=VMEM_BYTES),
    )(*operands)
    shape = (CX, CY, NZ)
    decoded, residual = pl.pallas_call(
        deliver,
        name="deliver",
        out_shape=(field, field),
        in_specs=(vmem, vmem),
        out_specs=(any_space, any_space),
        scratch_shapes=[sem.DMA((2,))],
        compiler_params=pltpu.CompilerParams(vmem_limit_bytes=1 << 20),
    )(decoded, residual)
    return decoded.reshape(shape), residual.reshape(shape), rms[0, 0]


def solution(mesh):
    placed = (P(("px", "py"), None), P(("px", "py"), None), P("px", "py", None))
    return jax.shard_map(
        shards,
        mesh=mesh,
        in_specs=placed,
        out_specs=(P("px", "py", None), P("px", "py", None), P()),
        check_vma=False,
    )
```

time: 62.1 us -> 50.5 us (0.81)
  Pallas kernels: 55.3 us -> 48 us
  local copies, waits for them, and re-layouts: 5.97 us -> 0 us
  between operations: 0.64 us -> 2.4 us
    pallas_call x1, Pallas kernels: 55.3 us -> 45.8 us  [shards(): pl.pallas_call(kernel, name='exchange', out_shape=(field, field, jax.Shap...]
    unnamed x4 -> x0, local copies, waits for them, and re-layouts: 4.79 us -> none
    pallas_call x0 -> x1, Pallas kernels: none -> 2.2 us  [shards(): pl.pallas_call(deliver, name='deliver', out_shape=(field, field), in_spec...]
    slice x1 -> x0, local copies, waits for them, and re-layouts: 1.18 us -> none  [shards(): return (decoded.reshape(shape), residual.reshape(shape), rms[0, 0])]
where the time goes in v2:
time: 50.5 us; the launch traced here: 50.4 us
  Pallas kernels  48 us (95%)
  between operations  2.4 us (5%)
    pallas_call x1, Pallas kernels, shards(): pl.pallas_call(kernel, name='exchange', out_shape=(field, field, jax.Shap...  45.8 us
    pallas_call x1, Pallas kernels, shards(): pl.pallas_call(deliver, name='deliver', out_shape=(field, field), in_spec...  2.2 us

profile of v2, /device:TPU:1, one launch (start us, length us, event | category | flops | bytes accessed | tf_op | source)
XLA Modules:
  0.0 50.4 jit_solution(1682888031276558670)
XLA Ops:
  0.6 45.8 %exchange.1 = (f32[384,1536]{1,0:T(8,128)S(1)}, f32[384,1536]{1,0:T(8,128)S(1)}, f32[1,1]{1,0:T(1,128)}) custom-call(bf16[12,49152]{1,0:T(8,128)(2,1)} %coef_hbm.1, s32[3,3072]{1,0:T(4,128)} %expo_hbm.1, f32[384,1536]{1,0:T(8,128)} %bitcast.4, bf16[384,384]{1,0:T(8,128)(2,1)} %constant.14.clone.spread_hbm, bf16[384,512]{1,0:T(8,128)(2,1)} %constant.15.clone.edge_hbm, ...), custom_call_target="tpu_custom_call" | custom-call | tf_op jit(solution)/shard_map/exchange/pallas_call | solution.py:482
  46.5 2.2 %deliver.1 = (f32[384,1536]{1,0:T(8,128)}, f32[384,1536]{1,0:T(8,128)}) custom-call(f32[384,1536]{1,0:T(8,128)S(1)} %get-tuple-element.8.dec_ref, f32[384,1536]{1,0:T(8,128)S(1)} %get-tuple-element.9.res_ref), custom_call_target="tpu_custom_call" | custom-call | tf_op jit(solution)/shard_map/deliver/pallas_call | solution.py:511

commit v3 on v2

--- a/solution.py
+++ b/solution.py
@@ -1,4 +1,4 @@
-import functools
+import random
 
 import jax
 import jax.numpy as jnp
@@ -14,11 +14,11 @@
 NZ = 1536
 PEERS = 128
 LAYERS = 12
+CHUNK = CELLS * PEERS // 4
 ROWS = 16
 F32 = jnp.float32
 BF16 = jnp.bfloat16
 MESH = pl.DeviceIdType.MESH
-UNROLL = 2
 VMEM_BYTES = 40 << 20
 
 
@@ -121,6 +121,13 @@
     return ((j >> 1) & 1) * 2 + (i & 1), i >> 1, j >> 2, j & 1
 
 
+def orders():
+    every = [(i, j, k, m) for k in range(4) for j in range(4) for i in range(4) for m in range(2)]
+    every = every[1:] if every[0] == (0, 0, 0, 0) else every
+    random.Random(0).shuffle(every)
+    return [[d for d in every if d[0] % 2 == phase % 2 and d[1] % 2 == phase // 2] for phase in range(4)]
+
+
 class Peers:
     def __init__(self):
         x, y, z, c = position()
@@ -149,29 +156,42 @@
     dec_ref, res_ref, rms_ref,
     coef, expo, right, spread, edge, part_of, turn, left, depth, place,
     sbuf, rbuf, ebuf, dpad, ext, pair_out, pair_in, part, parts,
-    load_sem, step_sem, send_sem, recv_sem, pair_send, pair_recv, sum_send, sum_recv,
+    load_sem, send_sem, recv_sem, pair_send, pair_recv, sum_send, sum_recv,
 ):
     x, y, z, c = position()
     peers = Peers()
     me = lax.axis_index("px") * 16 + lax.axis_index("py")
-    loads = [
-        pltpu.make_async_copy(src, dst, load_sem.at[n])
-        for n, (src, dst) in enumerate(
-            (
-                (coef_hbm, coef), (expo_hbm, expo), (spread_hbm, spread), (edge_hbm, edge), (part_hbm, part_of),
-                (turn_hbm, turn), (left_hbm, left), (depth_hbm, depth), (place_hbm, place), (right_hbm, right),
-            )
-        )
+    def load(n, src, dst):
+        return pltpu.make_async_copy(src, dst, load_sem.at[n])
+
+    chunks = [
+        load(n, coef_hbm.at[:, pl.ds(n * CHUNK, CHUNK)], coef.at[:, pl.ds(n * CHUNK, CHUNK)])
+        for n in range(4)
     ]
-    for load in loads:
-        load.start()
+    first = [load(4, expo_hbm, expo), load(5, spread_hbm, spread)]
+    second = [load(6, edge_hbm, edge), load(7, part_hbm, part_of), load(8, turn_hbm, turn)]
+    third = [load(9, left_hbm, left), load(10, depth_hbm, depth), load(11, place_hbm, place)]
+    third.append(load(12, right_hbm, right))
+    for copy in [*first, *chunks, *second]:
+        copy.start()
 
     entry = pltpu.get_barrier_semaphore()
-    for n in range(1, 8):
-        pl.semaphore_signal(entry, inc=1, device_id=ident(peers.at(n // 2, 0, 0, n % 2)), device_id_type=MESH)
-    for n in range(1, 4):
-        pl.semaphore_signal(entry, inc=1, device_id=ident(peers.at(0, n, 0, 0)), device_id_type=MESH)
-        pl.semaphore_signal(entry, inc=1, device_id=ident(peers.at(0, 0, n, 0)), device_id_type=MESH)
+    def everywhere(act):
+        def one(i, _):
+            for j in range(8):
+                def go(j=j):
+                    act(ident(peers.at((2, 1, 3, 0)[j >> 1], i + 2, (i >> 2) + 2, 1 - (j & 1))))
+
+                if j == 7:
+                    pl.when(i != 10)(go)
+                else:
+                    go()
+            return 0
+
+        lax.fori_loop(0, 16, one, 0)
+
+    with jax.named_scope("s_signal"):
+        everywhere(lambda there: pl.semaphore_signal(entry, inc=1, device_id=there, device_id_type=MESH))
 
     def clear(g, _):
         sbuf[pl.ds(g * 16, 16), 8:16, :] = jnp.zeros((16, 8, CELLS), BF16)
@@ -184,61 +204,60 @@
     ebuf[9] = jnp.zeros((18, 8, 256), F32)
 
     with jax.named_scope("s_load"):
-        for load in loads[:6]:
-            load.wait()
+        for copy in first:
+            copy.wait()
 
     row16 = lax.broadcasted_iota(jnp.int32, (ROWS, CELLS), 0)
     owner = lax.broadcasted_iota(jnp.int32, (ROWS, CELLS), 1) // 24
     upper = lax.broadcasted_iota(jnp.int32, (16, 8, 256), 1) < 4
 
-    def scale(g, _):
-        base = pl.multiple_of(g * 384, 128)
-        power = jnp.exp2(expo[:, pl.ds(base, 384)].astype(F32))
-        rows = jnp.where(row16 < 4, power[0:1], jnp.where(row16 < 8, power[1:2], power[2:3]))
-        apart = jnp.concatenate([jnp.where(owner == j, rows, 0.0) for j in range(16)], axis=0).astype(BF16)
-        factor = dot(apart, spread[...])
-        for j in range(16):
-            at = pl.multiple_of(g * (16 * CELLS) + j * CELLS, 128)
-            held = coef[:, pl.ds(at, CELLS)].astype(F32)
-            sbuf[g * 16 + j, 0:LAYERS, :] = (held * factor[j * 16 : j * 16 + LAYERS]).astype(BF16)
-        return 0
-
-    def edges(g, _):
-        held = sbuf[pl.ds(g * 16, 16)].reshape(256, CELLS)
-        wide = dot(held, edge[...])
-        wide = (wide[:, :256] + wide[:, 256:]).reshape(16, ROWS, 256)
-        first, second = wide[:, :8], wide[:, 8:]
-        first_turned, second_turned = pltpu.roll(first, 4, 1), pltpu.roll(second, 4, 1)
+    def scale(h):
+        apart = []
+        for g in (2 * h, 2 * h + 1):
+            power = jnp.exp2(expo[:, g * 384 : g * 384 + 384].astype(F32))
+            rows = jnp.where(row16 < 4, power[0:1], jnp.where(row16 < 8, power[1:2], power[2:3]))
+            apart += [jnp.where(owner == j, rows, 0.0) for j in range(16)]
+        factor = dot(jnp.concatenate(apart, axis=0).astype(BF16), spread[...])
+        for j in range(32):
+            at = (h * 32 + j) * CELLS
+            held = coef[:, at : at + CELLS].astype(F32)
+            sbuf[h * 32 + j, 0:LAYERS, :] = (held * factor[j * 16 : j * 16 + LAYERS]).astype(BF16)
+
+    def edges(h):
+        held = sbuf[h * 32 : h * 32 + 32].reshape(512, CELLS)
+        both = dot(held, edge[...])
+        both = (both[:, :256] + both[:, 256:]).reshape(32, ROWS, 256)
         kind = part_of[...][None]
-        four = jnp.where(
-            kind == 0,
-            jnp.where(upper, first, first_turned),
-            jnp.where(
-                kind == 1, jnp.where(upper, first_turned, first), jnp.where(upper, second, second_turned)
-            ),
-        )
         weights = [jnp.concatenate([turn[s], turn[s]], axis=1)[None] for s in range(4)]
-        mixed = four * weights[0]
-        for s in range(1, 4):
-            mixed = mixed + pltpu.roll(four, 8 - s, 1) * weights[s]
-        ebuf[g + 1, 1:17] = mixed
-        return 0
+        for n in range(2):
+            wide = both[n * 16 : n * 16 + 16]
+            first, second = wide[:, :8], wide[:, 8:]
+            first_turned, second_turned = pltpu.roll(first, 4, 1), pltpu.roll(second, 4, 1)
+            four = jnp.where(
+                kind == 0,
+                jnp.where(upper, first, first_turned),
+                jnp.where(
+                    kind == 1, jnp.where(upper, first_turned, first), jnp.where(upper, second, second_turned)
+                ),
+            )
+            mixed = four * weights[0]
+            for s in range(1, 4):
+                mixed = mixed + pltpu.roll(four, 8 - s, 1) * weights[s]
+            ebuf[h * 2 + n + 1, 1:17] = mixed
 
     with jax.named_scope("s_scale"):
-        lax.fori_loop(0, 8, scale, 0, unroll=UNROLL)
-
-    with jax.named_scope("s_bar1"):
-        pl.semaphore_wait(entry, 13)
-    for n in range(1, 4):
-        pl.semaphore_signal(step_sem.at[0], inc=1, device_id=ident(peers.at(0, n, 0, 0)), device_id_type=MESH)
+        for h in range(4):
+            chunks[h].wait()
+            scale(h)
+
+    for copy in third:
+        copy.start()
+    for copy in second:
+        copy.wait()
 
     with jax.named_scope("s_edges"):
-        lax.fori_loop(0, 8, edges, 0, unroll=UNROLL)
-
-    with jax.named_scope("s_bar2"):
-        pl.semaphore_wait(step_sem.at[0], 3)
-    for n in range(1, 4):
-        pl.semaphore_signal(step_sem.at[1], inc=1, device_id=ident(peers.at(0, 0, n, 0)), device_id_type=MESH)
+        for h in range(4):
+            edges(h)
 
     lane = lax.broadcasted_iota(jnp.int32, (16, 8, 256), 2)
     low = lane % 48 < 24
@@ -246,7 +265,10 @@
     half = lax.broadcasted_iota(jnp.int32, (16, 8, 128), 2) < 64
     even = lax.broadcasted_iota(jnp.int32, (16, 8, 128), 0) % 2 == 0
 
-    def gather(g, _):
+    def layer(parity, k):
+        return (y + parity + 2 * k) & 3
+
+    def gather(g):
         value = jnp.where(low, ebuf[g + 2, 1:17], ebuf[g, 1:17])
         along = jnp.where(even, pltpu.roll(ebuf[g + 1, 0:16, :, 128:], 80, 2), ebuf[g + 1, 2:18, :, 128:])
         one = value[:, :, :128]
@@ -258,38 +280,35 @@
         line = jnp.concatenate([one_hi, jnp.where(half, two_hi, first), jnp.where(half, first, second)], axis=2)
         tall = jnp.concatenate([jnp.zeros((16, 8, CELLS), F32), line], axis=1).astype(BF16)
         sbuf[pl.ds(g * 16, 16)] = sbuf[pl.ds(g * 16, 16)] + tall
-        return 0
+
+    def collect(phase):
+        for k in range(2):
+            gather(layer(phase // 2, k) * 2 + ((x + phase) & 1))
+
+    def start(phase):
+        for distance in orders()[phase]:
+            there = peers.at(*distance)
+            pltpu.make_async_remote_copy(
+                sbuf.at[there[0] * 16 + there[1]], rbuf.at[me], send_sem, recv_sem.at[phase],
+                device_id=ident(there), device_id_type=MESH,
+            ).start()
 
     with jax.named_scope("s_gather"):
-        lax.fori_loop(0, 8, gather, 0)
-    rbuf[me] = sbuf[me]
-    with jax.named_scope("s_bar3"):
-        pl.semaphore_wait(step_sem.at[1], 3)
-
-    def start(phase):
-        def one(i, _):
-            for j in range(8):
-                def go(j=j):
-                    there = peers.at((j & 1) * 2 + phase % 2, (j >> 1 & 1) * 2 + phase // 2, i + j, j >> 2)
-                    pltpu.make_async_remote_copy(
-                        sbuf.at[there[0] * 16 + there[1]], rbuf.at[me], send_sem, recv_sem.at[phase],
-                        device_id=ident(there), device_id_type=MESH,
-                    ).start()
-
-                if phase == 0 and j == 0:
-                    pl.when(i > 0)(go)
-                else:
-                    go()
-            return 0
-
-        lax.fori_loop(0, 4, one, 0)
-
+        collect(0)
+        collect(1)
+    with jax.named_scope("s_bar"):
+        pl.semaphore_wait(entry, PEERS - 1)
     with jax.named_scope("s_start"):
-        for phase in range(4):
-            start(phase)
-
-    for load in loads[6:]:
-        load.wait()
+        start(0)
+        collect(2)
+        start(1)
+        collect(3)
+        start(2)
+        rbuf[me] = sbuf[me]
+        start(3)
+
+    for copy in third:
+        copy.wait()
 
     def wipe(n, _):
         dpad[n] = jnp.zeros((CY, NZ + 256), F32)
@@ -299,9 +318,6 @@
     ext[...] = jnp.zeros((CX, NZ), F32)
 
     here = ident(peers.at(0, 0, 0, 1))
-
-    def layer(parity, k):
-        return (y + parity + 2 * k) & 3
 
     def pair_copy(parity, k):
         at = pl.multiple_of(layer(parity, k) * 384, 128)
@@ -382,7 +398,7 @@
                 value = jnp.where((column > 0) & (column < 383), value, 0.0)
             return total + squares(value)
 
-        return lax.fori_loop(0, CX, slab, total, unroll=4)
+        return lax.fori_loop(0, CX, slab, total, unroll=8)
 
     def seam(k, total):
         at = layer(0, k) * 384
@@ -401,7 +417,7 @@
             res_ref[out, back] = value
             return total + squares(jnp.where(tile == 127, value, 0.0))
 
-        return lax.fori_loop(0, CX, slab, total, unroll=4)
+        return lax.fori_loop(0, CX, slab, total, unroll=8)
 
     total = jnp.zeros((8, 128), F32)
     for phase in range(4):
@@ -414,7 +430,7 @@
                 decode(phase, k)
                 if phase % 2 == 1:
                     pair_start(phase // 2, k)
-        if phase == 2:
+        if phase == 1:
             with jax.named_scope("s_early"):
                 for k in range(2):
                     pair_copy(0, k).wait()
@@ -432,37 +448,29 @@
     part[...] = jnp.sum(total, axis=0, keepdims=True)
     parts[me] = part[...]
 
-    def tell(i, _):
-        for j in range(8):
-            def go(j=j):
-                there = peers.at((2, 1, 3, 0)[j >> 1], i + 2, (i >> 2) + 2, 1 - (j & 1))
-                pltpu.make_async_remote_copy(
-                    part, parts.at[me], sum_send, sum_recv, device_id=ident(there), device_id_type=MESH
-                ).start()
-
-            if j == 7:
-                pl.when(i != 10)(go)
-            else:
-                go()
-        return 0
-
-    with jax.named_scope("s_tell"):
-        lax.fori_loop(0, 16, tell, 0)
     everyone = pl.ds(0, PEERS - 1)
     with jax.named_scope("s_sent"):
         pltpu.make_async_copy(sbuf.at[everyone], sbuf.at[everyone], send_sem).wait()
+    with jax.named_scope("s_tell"):
+        everywhere(
+            lambda there: pltpu.make_async_remote_copy(
+                part, parts.at[me], sum_send, sum_recv, device_id=there, device_id_type=MESH
+            ).start()
+        )
     with jax.named_scope("s_sum"):
         pltpu.make_async_copy(parts.at[everyone], parts.at[everyone], sum_recv).wait()
     pltpu.make_async_copy(parts.at[everyone], parts.at[everyone], sum_send).wait()
     whole = jnp.sum(jnp.sum(parts[...], axis=0), axis=1, keepdims=True)
-    rms_ref[0, 0] = jnp.sqrt(whole / (PEERS * CELLS * NZ) + 1e-06)[0, 0]
-
-
-def deliver(dec_ref, res_ref, dec_out, res_out, sems):
-    copies = [
-        pltpu.make_async_copy(src, dst, sems.at[n])
-        for n, (src, dst) in enumerate(((dec_ref, dec_out), (res_ref, res_out)))
-    ]
+    rms_ref[...] = jnp.sqrt(whole / (PEERS * CELLS * NZ) + 1e-06)
+
+
+def deliver(dec_ref, res_ref, rms_ref, dec_out, res_out, rms_out, sems):
+    copies = []
+    for src, dst in ((dec_ref, dec_out), (res_ref, res_out)):
+        for n in range(4):
+            rows = pl.ds(n * (CELLS // 4), CELLS // 4)
+            copies.append(pltpu.make_async_copy(src.at[rows], dst.at[rows], sems.at[len(copies)]))
+    copies.insert(0, pltpu.make_async_copy(rms_ref, rms_out, sems.at[8]))
     for copy in copies:
         copy.start()
     for copy in copies:
@@ -484,7 +492,7 @@
         name="exchange",
         out_shape=(field, field, jax.ShapeDtypeStruct((1, 1), F32)),
         in_specs=[any_space] * len(operands),
-        out_specs=(vmem, vmem, pl.BlockSpec(memory_space=pltpu.SMEM)),
+        out_specs=(vmem, vmem, vmem),
         scratch_shapes=[
             *held,
             pltpu.VMEM((PEERS, ROWS, CELLS), BF16),
@@ -496,8 +504,7 @@
             pltpu.VMEM((CX, NZ), F32),
             pltpu.VMEM((1, 128), F32),
             pltpu.VMEM((PEERS, 1, 128), F32),
-            sem.DMA((len(operands),)),
-            sem.REGULAR((2,)),
+            sem.DMA((13,)),
             sem.DMA,
             sem.DMA((4,)),
             sem.DMA((4,)),
@@ -508,15 +515,15 @@
         compiler_params=pltpu.CompilerParams(collective_id=0, has_side_effects=True, vmem_limit_bytes=VMEM_BYTES),
     )(*operands)
     shape = (CX, CY, NZ)
-    decoded, residual = pl.pallas_call(
+    decoded, residual, rms = pl.pallas_call(
         deliver,
         name="deliver",
-        out_shape=(field, field),
-        in_specs=(vmem, vmem),
-        out_specs=(any_space, any_space),
-        scratch_shapes=[sem.DMA((2,))],
+        out_shape=(field, field, jax.ShapeDtypeStruct((1, 1), F32)),
+        in_specs=(vmem, vmem, vmem),
+        out_specs=(any_space, any_space, any_space),
+        scratch_shapes=[sem.DMA((9,))],
         compiler_params=pltpu.CompilerParams(vmem_limit_bytes=1 << 20),
-    )(decoded, residual)
+    )(decoded, residual, rms)
     return decoded.reshape(shape), residual.reshape(shape), rms[0, 0]
 
 

time: 50.5 us -> 46.2 us (0.915)
  Pallas kernels: 48 us -> 45.5 us
  between operations: 2.4 us -> 0.64 us
    pallas_call x1, Pallas kernels: 45.8 us -> 42.6 us  [shards(): pl.pallas_call(kernel, name='exchange', out_shape=(field, field, jax.Shap...]
    pallas_call x1, Pallas kernels: 2.2 us -> 2.89 us  [shards(): pl.pallas_call(deliver, name='deliver', out_shape=(field, field, jax.Shap...]
where the time goes in v3:
time: 46.2 us; the launch traced here: 46.1 us
  Pallas kernels  45.5 us (98%)
  between operations  0.64 us (1%)
    pallas_call x1, Pallas kernels, shards(): pl.pallas_call(kernel, name='exchange', out_shape=(field, field, jax.Shap...  42.6 us
    pallas_call x1, Pallas kernels, shards(): pl.pallas_call(deliver, name='deliver', out_shape=(field, field, jax.Shap...  2.89 us

profile of v3, /device:TPU:1, one launch (start us, length us, event | category | flops | bytes accessed | tf_op | source)
XLA Modules:
  0.0 46.1 jit_solution(10266060064395002683)
XLA Ops:
  0.6 42.6 %exchange.1 = (f32[384,1536]{1,0:T(8,128)S(1)}, f32[384,1536]{1,0:T(8,128)S(1)}, f32[1,1]{1,0:T(1,128)}) custom-call(bf16[12,49152]{1,0:T(8,128)(2,1)} %coef_hbm.1, s32[3,3072]{1,0:T(4,128)} %expo_hbm.1, f32[384,1536]{1,0:T(8,128)} %bitcast.4, bf16[384,384]{1,0:T(8,128)(2,1)} %constant.14.clone.spread_hbm, bf16[384,512]{1,0:T(8,128)(2,1)} %constant.15.clone.edge_hbm, ...), custom_call_target="tpu_custom_call" | custom-call | tf_op jit(solution)/shard_map/exchange/pallas_call | solution.py:490
  43.2 2.9 %deliver.1 = (f32[384,1536]{1,0:T(8,128)}, f32[384,1536]{1,0:T(8,128)}, f32[1,1]{1,0:T(1,128)}) custom-call(f32[384,1536]{1,0:T(8,128)S(1)} %get-tuple-element.9.dec_ref, f32[384,1536]{1,0:T(8,128)S(1)} %get-tuple-element.10.res_ref, f32[1,1]{1,0:T(1,128)} %get-tuple-element.11.rms_ref), custom_call_target="tpu_custom_call" | custom-call | tf_op jit(solution)/shard_map/deliver/pallas_call | solution.py:518

commit v4 on v3

--- a/solution.py
+++ b/solution.py
@@ -33,6 +33,13 @@
     hi = table.astype(np.float32).astype(BF16)
     lo = (table - hi.astype(np.float64)).astype(np.float32).astype(BF16)
     return hi, lo
+
+
+def whole_basis():
+    b = basis()
+    p, q = 408 / 512, 169 / 512
+    gain = np.sqrt(b[1, 0] / p * b[1, 1] / q)
+    return np.stack([b[0], [p, q, -q, -p], b[2], [q, -p, p, -q]]), gain
 
 
 def block_table(width):
@@ -78,6 +85,7 @@
             np.concatenate([plane_hi[192:, 128:], plane_lo[192:, 128:], pick_lo]),
         ]
     )
+    whole, gain = whole_basis()
     depth = np.zeros((2, 256, 256))
     place = np.zeros((2, 768, 256))
     for odd in range(2):
@@ -85,20 +93,22 @@
             base = 64 * odd + s * LAYERS
             for z in range(LAYERS):
                 for o in range(z // 4 * 4, z // 4 * 4 + 4):
-                    depth[odd, s * 16 + z, base + o] = b[z % 4, o % 4]
+                    depth[odd, s * 16 + z, base + o] = whole[z % 4, o % 4]
             for k in range(3):
                 for r in range(4):
                     place[odd, k * 256 + s * 16 + 12 + r, base + k * 4 + r] = 1
-    depth_hi, depth_lo = halves(depth)
+    lift = np.broadcast_to(np.where(np.arange(256) % 2, gain, 1.0)[None, :], (8, 256)).astype(np.float32)
     column = np.arange(CELLS)
-    spread = (column[:, None] % 24 == (column[None, :] // CY // 4) * 6 + column[None, :] % CY // 4).astype(BF16)
+    spread = column[:, None] % 24 == (column[None, :] // CY // 4) * 6 + column[None, :] % CY // 4
+    spread = np.stack([spread[:256], spread[128:]]).astype(BF16)
     return (
         spread,
         np.concatenate([edge_hi, edge_lo], axis=1),
         part,
         turn,
         left,
-        np.stack([depth_hi, depth_lo], axis=1),
+        lift,
+        depth.astype(BF16),
         place.astype(BF16),
     )
 
@@ -125,7 +135,12 @@
     every = [(i, j, k, m) for k in range(4) for j in range(4) for i in range(4) for m in range(2)]
     every = every[1:] if every[0] == (0, 0, 0, 0) else every
     random.Random(0).shuffle(every)
+    every.sort(key=lambda d: -sum(min(v, 4 - v) for v in d[:3]))
     return [[d for d in every if d[0] % 2 == phase % 2 and d[1] % 2 == phase // 2] for phase in range(4)]
+
+
+def half_of(distance):
+    return (-distance[1] % 4 - distance[1] % 2) // 2
 
 
 class Peers:
@@ -152,9 +167,9 @@
 
 
 def kernel(
-    coef_hbm, expo_hbm, right_hbm, spread_hbm, edge_hbm, part_hbm, turn_hbm, left_hbm, depth_hbm, place_hbm,
-    dec_ref, res_ref, rms_ref,
-    coef, expo, right, spread, edge, part_of, turn, left, depth, place,
+    coef_hbm, expo_hbm, right_hbm, spread_hbm, edge_hbm, part_hbm, turn_hbm, left_hbm, lift_hbm, depth_hbm, place_hbm,
+    dec_ref, res_ref, sum_ref,
+    coef, expo, right, spread, edge, part_of, turn, left, lift, depth, place,
     sbuf, rbuf, ebuf, dpad, ext, pair_out, pair_in, part, parts,
     load_sem, send_sem, recv_sem, pair_send, pair_recv, sum_send, sum_recv,
 ):
@@ -171,7 +186,7 @@
     first = [load(4, expo_hbm, expo), load(5, spread_hbm, spread)]
     second = [load(6, edge_hbm, edge), load(7, part_hbm, part_of), load(8, turn_hbm, turn)]
     third = [load(9, left_hbm, left), load(10, depth_hbm, depth), load(11, place_hbm, place)]
-    third.append(load(12, right_hbm, right))
+    third += [load(12, lift_hbm, lift), load(13, right_hbm, right)]
     for copy in [*first, *chunks, *second]:
         copy.start()
 
@@ -207,21 +222,29 @@
         for copy in first:
             copy.wait()
 
-    row16 = lax.broadcasted_iota(jnp.int32, (ROWS, CELLS), 0)
-    owner = lax.broadcasted_iota(jnp.int32, (ROWS, CELLS), 1) // 24
+    row8 = lax.broadcasted_iota(jnp.int32, (8, 256), 0)
+    lane8 = lax.broadcasted_iota(jnp.int32, (8, 256), 1)
+    row12 = lax.broadcasted_iota(jnp.int32, (LAYERS, CELLS), 0)
+    owners = (lane8 // 24, (lane8 + 128) // 24)
     upper = lax.broadcasted_iota(jnp.int32, (16, 8, 256), 1) < 4
 
     def scale(h):
-        apart = []
-        for g in (2 * h, 2 * h + 1):
-            power = jnp.exp2(expo[:, g * 384 : g * 384 + 384].astype(F32))
-            rows = jnp.where(row16 < 4, power[0:1], jnp.where(row16 < 8, power[1:2], power[2:3]))
-            apart += [jnp.where(owner == j, rows, 0.0) for j in range(16)]
-        factor = dot(jnp.concatenate(apart, axis=0).astype(BF16), spread[...])
+        factors = []
+        for n in range(2):
+            apart = []
+            for g in (2 * h, 2 * h + 1):
+                at = g * 384 + n * 128
+                power = jnp.exp2(expo[:, at : at + 256].astype(F32))
+                rows = jnp.where(row8 % 4 == 0, power[0:1], jnp.where(row8 % 4 == 1, power[1:2], power[2:3]))
+                apart += [jnp.where(owners[n] == n * 8 + j + row8 // 4, rows, 0.0) for j in range(0, 8, 2)]
+            factors.append(dot(jnp.concatenate(apart, axis=0).astype(BF16), spread[n]))
         for j in range(32):
             at = (h * 32 + j) * CELLS
             held = coef[:, at : at + CELLS].astype(F32)
-            sbuf[h * 32 + j, 0:LAYERS, :] = (held * factor[j * 16 : j * 16 + LAYERS]).astype(BF16)
+            row = (j // 16 * 8 + j % 8) * 4
+            some = factors[j // 8 % 2][row : row + 3]
+            factor = jnp.where(row12 < 4, some[0:1], jnp.where(row12 < 8, some[1:2], some[2:3]))
+            sbuf[h * 32 + j, 0:LAYERS, :] = (held * factor).astype(BF16)
 
     def edges(h):
         held = sbuf[h * 32 : h * 32 + 32].reshape(512, CELLS)
@@ -289,7 +312,7 @@
         for distance in orders()[phase]:
             there = peers.at(*distance)
             pltpu.make_async_remote_copy(
-                sbuf.at[there[0] * 16 + there[1]], rbuf.at[me], send_sem, recv_sem.at[phase],
+                sbuf.at[there[0] * 16 + there[1]], rbuf.at[me], send_sem, recv_sem.at[phase * 2 + half_of(distance)],
                 device_id=ident(there), device_id_type=MESH,
             ).start()
 
@@ -335,25 +358,28 @@
         pair_out[:, pl.ds(pl.multiple_of(at, 128), 384)] = jnp.where(c == 0, last, first)
         pair_copy(parity, k).start()
 
-    def decode(phase, k):
+    def decode(phase, ks):
         odd = (x + phase) & 1
-        group = layer(phase // 2, k) * 2 + odd
-        at = layer(phase // 2, k) * 384 + odd * 128
-        held = rbuf[pl.ds(group * 16, 16)].reshape(256, CELLS)
-        near = dot_rows(left[0], held[:, :256])
-        far = dot_rows(left[1], held[:, 128:])
-        hi, lo = two(jnp.concatenate([near[:192] + near[192:384], far[:192] + far[192:384]], axis=0))
-        table = depth[odd, 0]
-        field = dot(hi, table) + dot(lo, table) + dot(hi, depth[odd, 1])
-        side_hi = jnp.concatenate([near[384:448], near[448:512], near[512:576]], axis=1).astype(BF16)
-        side_lo = jnp.concatenate([far[384:448], far[448:512], far[512:576]], axis=1).astype(BF16)
-        table = place[odd]
-        side = dot(side_hi, table) + dot(side_lo, table)
-        lanes = pl.ds(pl.multiple_of(at + 128, 128), 256)
-        dpad[1 : CX + 1, :, lanes] += field.reshape(CX, CY, 256)
-        dpad[0, :, lanes] += side[24:48]
-        dpad[CX + 1, :, lanes] += side[0:24]
-        ext[:, pl.ds(pl.multiple_of(at, 128), 256)] += side[48:64]
+        wides = []
+        for k in ks:
+            held = rbuf[pl.ds((layer(phase // 2, k) * 2 + odd) * 16, 16)].reshape(256, CELLS)
+            wides.append((dot_rows(left[0], held[:, :256]), dot_rows(left[1], held[:, 128:])))
+        for k, (near, far) in zip(ks, wides):
+            across = jnp.concatenate([near[:192] + near[192:384], far[:192] + far[192:384]], axis=0)
+            hi, lo = two(across * lift[0:1, :])
+            field = dot(hi, depth[odd]) + dot(lo, depth[odd])
+            side_hi = jnp.concatenate([near[384:448], near[448:512], near[512:576]], axis=1).astype(BF16)
+            side_lo = jnp.concatenate([far[384:448], far[448:512], far[512:576]], axis=1).astype(BF16)
+            side = dot(jnp.concatenate([side_hi, side_lo], axis=0), place[odd])
+            side = side[:64] + side[64:]
+            at = layer(phase // 2, k) * 384 + odd * 128
+            lanes = pl.ds(pl.multiple_of(at + 128, 128), 256)
+            dpad[1 : CX + 1, :, lanes] += field.reshape(CX, CY, 256)
+            dpad[0, :, lanes] += side[24:48]
+            dpad[CX + 1, :, lanes] += side[0:24]
+            ext[:, pl.ds(pl.multiple_of(at, 128), 256)] += side[48:64]
+            if phase % 2 == 1:
+                pair_start(phase // 2, k)
 
     column = lax.broadcasted_iota(jnp.int32, (CY, 384), 1)
     row = lax.broadcasted_iota(jnp.int32, (CY, 384), 0)
@@ -365,12 +391,16 @@
         return sum(value[:, k * 128 : (k + 1) * 128] for k in range(value.shape[1] // 128))
 
     def residual(parity, k, total):
-        at = layer(parity, k) * 384
+        depth_at = layer(parity, k)
+        at = depth_at * 384
         lanes = pl.ds(pl.multiple_of(at, 128), 384)
         inside = pl.ds(pl.multiple_of(at + 128, 128), 384)
+        low_at = jnp.maximum(at - 128, 0)
+        high_at = jnp.minimum(at + 384, NZ - 128)
+        counted = ((column > 0) | (depth_at == 0)) & ((column < 383) | (depth_at == 3))
 
         def slab(n, total):
-            rows = pl.multiple_of(n * CY, 8)
+            rows = pl.ds(pl.multiple_of(n * CY, 8), CY)
             own = dpad[n + 1, :, inside]
             near = dpad[n, :, inside] + dpad[n + 2, :, inside]
             inner, outer = pair_in[pl.ds(n, 1), lanes], ext[pl.ds(n, 1), lanes]
@@ -385,64 +415,56 @@
             else:
                 prior = dpad[n + 1, :, pl.ds(pl.multiple_of(at, 128), 128)]
                 later = dpad[n + 1, :, pl.ds(pl.multiple_of(at + 512, 128), 128)]
-                back = jnp.concatenate(
-                    [jnp.where(tile == 0, pltpu.roll(prior, 1, 1), back[:, :128]), back[:, 128:]], axis=1
+                first, last = back[:, :128], forth[:, 256:]
+                back = jnp.concatenate([jnp.where(tile == 0, pltpu.roll(prior, 1, 1), first), back[:, 128:]], axis=1)
+                forth = jnp.concatenate(
+                    [forth[:, :256], jnp.where(tile == 127, pltpu.roll(later, 127, 1), last)], axis=1
                 )
-                forth = jnp.concatenate(
-                    [forth[:, :256], jnp.where(tile == 127, pltpu.roll(later, 127, 1), forth[:, 256:])], axis=1
-                )
-            value = right[pl.ds(rows, CY), lanes] - (6.0 * own - (near + back + forth))
-            dec_ref[pl.ds(rows, CY), lanes] = own
-            res_ref[pl.ds(rows, CY), lanes] = value
+            value = right[rows, lanes] - (6.0 * own - (near + back + forth))
+            dec_ref[rows, lanes] = own
+            res_ref[rows, lanes] = value
             if parity == 0:
-                value = jnp.where((column > 0) & (column < 383), value, 0.0)
-            return total + squares(value)
-
-        return lax.fori_loop(0, CX, slab, total, unroll=8)
-
-    def seam(k, total):
-        at = layer(0, k) * 384
-
-        def slab(n, total):
-            rows = pl.multiple_of(n * CY, 8)
-            out = pl.ds(rows, CY)
-            front = pl.ds(pl.multiple_of(at, 128), 128)
-            prior = pltpu.roll(dpad[n + 1, :, front], 1, 1)
-            value = res_ref[out, front] + jnp.where(tile == 0, prior, 0.0)
-            res_ref[out, front] = value
-            total = total + squares(jnp.where(tile == 0, value, 0.0))
-            back = pl.ds(pl.multiple_of(at + 256, 128), 128)
-            later = pltpu.roll(dpad[n + 1, :, pl.ds(pl.multiple_of(at + 512, 128), 128)], 127, 1)
-            value = res_ref[out, back] + jnp.where(tile == 127, later, 0.0)
-            res_ref[out, back] = value
-            return total + squares(jnp.where(tile == 127, value, 0.0))
+                return total + squares(jnp.where(counted, value, 0.0))
+            total = total + squares(value)
+            for there, edge_lane, carried, exists in (
+                (low_at, 127, last, depth_at > 0),
+                (high_at, 0, first, depth_at < 3),
+            ):
+                spot = pl.ds(pl.multiple_of(there, 128), 128)
+                mine = (tile == edge_lane) & exists
+                value = res_ref[rows, spot] + jnp.where(mine, carried, 0.0)
+                res_ref[rows, spot] = value
+                total = total + squares(jnp.where(mine, value, 0.0))
+            return total
 
         return lax.fori_loop(0, CX, slab, total, unroll=8)
 
     total = jnp.zeros((8, 128), F32)
     for phase in range(4):
-        count = 32 - (phase == 0)
-        block = rbuf.at[pl.ds(0, count)]
-        with jax.named_scope("s_wait"):
-            pltpu.make_async_copy(block, block, recv_sem.at[phase]).wait()
-        with jax.named_scope("s_decode"):
+        def arrive(k):
+            block = rbuf.at[pl.ds(0, 16 - (phase == 0 and k == 0))]
+            with jax.named_scope("s_wait"):
+                pltpu.make_async_copy(block, block, recv_sem.at[phase * 2 + k]).wait()
+
+        if phase == 3:
+            arrive(0)
+            arrive(1)
+            with jax.named_scope("s_decode"):
+                decode(phase, (0, 1))
+        else:
             for k in range(2):
-                decode(phase, k)
-                if phase % 2 == 1:
-                    pair_start(phase // 2, k)
+                arrive(k)
+                with jax.named_scope("s_decode"):
+                    decode(phase, (k,))
         if phase == 1:
             with jax.named_scope("s_early"):
                 for k in range(2):
                     pair_copy(0, k).wait()
                     total = residual(0, k, total)
-    with jax.named_scope("s_seam"):
-        for k in range(2):
-            total = seam(k, total)
-    with jax.named_scope("s_pair"):
-        for k in range(2):
+    for k in range(2):
+        with jax.named_scope("s_pair"):
             pair_copy(1, k).wait()
-    with jax.named_scope("s_late"):
-        for k in range(2):
+        with jax.named_scope("s_late"):
             total = residual(1, k, total)
 
     part[...] = jnp.sum(total, axis=0, keepdims=True)
@@ -460,19 +482,19 @@
     with jax.named_scope("s_sum"):
         pltpu.make_async_copy(parts.at[everyone], parts.at[everyone], sum_recv).wait()
     pltpu.make_async_copy(parts.at[everyone], parts.at[everyone], sum_send).wait()
-    whole = jnp.sum(jnp.sum(parts[...], axis=0), axis=1, keepdims=True)
-    rms_ref[...] = jnp.sqrt(whole / (PEERS * CELLS * NZ) + 1e-06)
-
-
-def deliver(dec_ref, res_ref, rms_ref, dec_out, res_out, rms_out, sems):
-    copies = []
-    for src, dst in ((dec_ref, dec_out), (res_ref, res_out)):
-        for n in range(4):
-            rows = pl.ds(n * (CELLS // 4), CELLS // 4)
-            copies.append(pltpu.make_async_copy(src.at[rows], dst.at[rows], sems.at[len(copies)]))
-    copies.insert(0, pltpu.make_async_copy(rms_ref, rms_out, sems.at[8]))
-    for copy in copies:
-        copy.start()
+    sum_ref[...] = jnp.broadcast_to(jnp.sum(parts[...], axis=0), (8, 128))
+
+
+def deliver(dec_ref, res_ref, sum_ref, dec_out, res_out, rms_out, rms, sems):
+    copies = [
+        pltpu.make_async_copy(src, dst, sems.at[n])
+        for n, (src, dst) in enumerate(((dec_ref, dec_out), (res_ref, res_out), (rms, rms_out)))
+    ]
+    copies[0].start()
+    copies[1].start()
+    whole = jnp.sum(sum_ref[0:1, :], axis=1, keepdims=True)
+    rms[...] = jnp.sqrt(whole / (PEERS * CELLS * NZ) + 1e-06)
+    copies[2].start()
     for copy in copies:
         copy.wait()
 
@@ -487,10 +509,10 @@
     held = [pltpu.VMEM(o.shape, o.dtype) for o in operands]
     sem = pltpu.SemaphoreType
     field = jax.ShapeDtypeStruct((CELLS, NZ), F32)
-    decoded, residual, rms = pl.pallas_call(
+    decoded, residual, total = pl.pallas_call(
         kernel,
         name="exchange",
-        out_shape=(field, field, jax.ShapeDtypeStruct((1, 1), F32)),
+        out_shape=(field, field, jax.ShapeDtypeStruct((8, 128), F32)),
         in_specs=[any_space] * len(operands),
         out_specs=(vmem, vmem, vmem),
         scratch_shapes=[
@@ -504,9 +526,9 @@
             pltpu.VMEM((CX, NZ), F32),
             pltpu.VMEM((1, 128), F32),
             pltpu.VMEM((PEERS, 1, 128), F32),
-            sem.DMA((13,)),
+            sem.DMA((14,)),
             sem.DMA,
-            sem.DMA((4,)),
+            sem.DMA((8,)),
             sem.DMA((4,)),
             sem.DMA((4,)),
             sem.DMA,
@@ -521,9 +543,9 @@
         out_shape=(field, field, jax.ShapeDtypeStruct((1, 1), F32)),
         in_specs=(vmem, vmem, vmem),
         out_specs=(any_space, any_space, any_space),
-        scratch_shapes=[sem.DMA((9,))],
+        scratch_shapes=[pltpu.VMEM((1, 1), F32), sem.DMA((3,))],
         compiler_params=pltpu.CompilerParams(vmem_limit_bytes=1 << 20),
-    )(decoded, residual, rms)
+    )(decoded, residual, total)
     return decoded.reshape(shape), residual.reshape(shape), rms[0, 0]
 
 

time: 46.2 us -> 43.7 us (0.946)
  Pallas kernels: 45.5 us -> 43 us
    pallas_call x1, Pallas kernels: 42.6 us -> 40.8 us  [shards(): pl.pallas_call(kernel, name='exchange', out_shape=(field, field, jax.Shap...]
    pallas_call x1, Pallas kernels: 2.89 us -> 2.21 us  [shards(): pl.pallas_call(deliver, name='deliver', out_shape=(field, field, jax.Shap...]
where the time goes in v4:
time: 43.7 us; the launch traced here: 43.6 us
  Pallas kernels  43 us (98%)
  between operations  0.64 us (1%)
    pallas_call x1, Pallas kernels, shards(): pl.pallas_call(kernel, name='exchange', out_shape=(field, field, jax.Shap...  40.8 us
    pallas_call x1, Pallas kernels, shards(): pl.pallas_call(deliver, name='deliver', out_shape=(field, field, jax.Shap...  2.21 us

profile of v4, /device:TPU:1, one launch (start us, length us, event | category | flops | bytes accessed | tf_op | source)
XLA Modules:
  0.0 43.6 jit_solution(3882771687051233184)
XLA Ops:
  0.6 40.8 %exchange.1 = (f32[384,1536]{1,0:T(8,128)S(1)}, f32[384,1536]{1,0:T(8,128)S(1)}, f32[8,128]{1,0:T(8,128)S(1)}) custom-call(bf16[12,49152]{1,0:T(8,128)(2,1)} %coef_hbm.1, s32[3,3072]{1,0:T(4,128)} %expo_hbm.1, f32[384,1536]{1,0:T(8,128)} %bitcast.4, bf16[2,256,384]{2,1,0:T(8,128)(2,1)} %constant.16.clone.spread_hbm, ...), custom_call_target="tpu_custom_call" | custom-call | tf_op jit(solution)/shard_map/exchange/pallas_call | solution.py:512
  41.4 2.2 %deliver.1 = (f32[384,1536]{1,0:T(8,128)}, f32[384,1536]{1,0:T(8,128)}, f32[1,1]{1,0:T(1,128)}) custom-call(f32[384,1536]{1,0:T(8,128)S(1)} %get-tuple-element.9.dec_ref, f32[384,1536]{1,0:T(8,128)S(1)} %get-tuple-element.10.res_ref, f32[8,128]{1,0:T(8,128)S(1)} %get-tuple-element.11.sum_ref), custom_call_target="tpu_custom_call" | custom-call | tf_op jit(solution)/shard_map/deliver/pallas_call | solution.py:540

commit v5 on v4

--- a/solution.py
+++ b/solution.py
@@ -192,18 +192,8 @@
 
     entry = pltpu.get_barrier_semaphore()
     def everywhere(act):
-        def one(i, _):
-            for j in range(8):
-                def go(j=j):
-                    act(ident(peers.at((2, 1, 3, 0)[j >> 1], i + 2, (i >> 2) + 2, 1 - (j & 1))))
-
-                if j == 7:
-                    pl.when(i != 10)(go)
-                else:
-                    go()
-            return 0
-
-        lax.fori_loop(0, 16, one, 0)
+        for distance in sorted(sum(orders(), []), key=lambda d: -sum(min(v, 4 - v) for v in d[:3])):
+            act(ident(peers.at(*distance)))
 
     with jax.named_scope("s_signal"):
         everywhere(lambda there: pl.semaphore_signal(entry, inc=1, device_id=there, device_id_type=MESH))

time: 43.7 us -> 42.4 us (0.970)
  Pallas kernels: 43 us -> 41.6 us
    pallas_call x1, Pallas kernels: 40.8 us -> 39.4 us  [shards(): pl.pallas_call(kernel, name='exchange', out_shape=(field, field, jax.Shap...]
where the time goes in v5:
time: 42.4 us; the launch traced here: 42.3 us
  Pallas kernels  41.6 us (98%)
  between operations  0.64 us (2%)
    pallas_call x1, Pallas kernels, shards(): pl.pallas_call(kernel, name='exchange', out_shape=(field, field, jax.Shap...  39.4 us
    pallas_call x1, Pallas kernels, shards(): pl.pallas_call(deliver, name='deliver', out_shape=(field, field, jax.Shap...  2.21 us

profile of v5, /device:TPU:1, one launch (start us, length us, event | category | flops | bytes accessed | tf_op | source)
XLA Modules:
  0.0 42.3 jit_solution(17666961281126334975)
XLA Ops:
  0.6 39.4 %exchange.1 = (f32[384,1536]{1,0:T(8,128)S(1)}, f32[384,1536]{1,0:T(8,128)S(1)}, f32[8,128]{1,0:T(8,128)S(1)}) custom-call(bf16[12,49152]{1,0:T(8,128)(2,1)} %coef_hbm.1, s32[3,3072]{1,0:T(4,128)} %expo_hbm.1, f32[384,1536]{1,0:T(8,128)} %bitcast.4, bf16[2,256,384]{2,1,0:T(8,128)(2,1)} %constant.16.clone.spread_hbm, ...), custom_call_target="tpu_custom_call" | custom-call | tf_op jit(solution)/shard_map/exchange/pallas_call | solution.py:502
  40.1 2.2 %deliver.1 = (f32[384,1536]{1,0:T(8,128)}, f32[384,1536]{1,0:T(8,128)}, f32[1,1]{1,0:T(1,128)}) custom-call(f32[384,1536]{1,0:T(8,128)S(1)} %get-tuple-element.9.dec_ref, f32[384,1536]{1,0:T(8,128)S(1)} %get-tuple-element.10.res_ref, f32[8,128]{1,0:T(8,128)S(1)} %get-tuple-element.11.sum_ref), custom_call_target="tpu_custom_call" | custom-call | tf_op jit(solution)/shard_map/deliver/pallas_call | solution.py:530

commit v6 on v5

--- a/solution.py
+++ b/solution.py
@@ -307,18 +307,14 @@
             ).start()
 
     with jax.named_scope("s_gather"):
-        collect(0)
-        collect(1)
+        for phase in range(4):
+            collect(phase)
     with jax.named_scope("s_bar"):
         pl.semaphore_wait(entry, PEERS - 1)
     with jax.named_scope("s_start"):
-        start(0)
-        collect(2)
-        start(1)
-        collect(3)
-        start(2)
-        rbuf[me] = sbuf[me]
-        start(3)
+        for phase in range(4):
+            start(phase)
+    rbuf[me] = sbuf[me]
 
     for copy in third:
         copy.wait()

time: 42.4 us -> 42.4 us (level)
  no operation moved by 1% of the time
where the time goes in v6:
time: 42.4 us; the launch traced here: 42.3 us
  Pallas kernels  41.6 us (98%)
  between operations  0.64 us (2%)
    pallas_call x1, Pallas kernels, shards(): pl.pallas_call(kernel, name='exchange', out_shape=(field, field, jax.Shap...  39.4 us
    pallas_call x1, Pallas kernels, shards(): pl.pallas_call(deliver, name='deliver', out_shape=(field, field, jax.Shap...  2.21 us

profile of v6, /device:TPU:1, one launch (start us, length us, event | category | flops | bytes accessed | tf_op | source)
XLA Modules:
  0.0 42.3 jit_solution(7677896999950777656)
XLA Ops:
  0.6 39.4 %exchange.1 = (f32[384,1536]{1,0:T(8,128)S(1)}, f32[384,1536]{1,0:T(8,128)S(1)}, f32[8,128]{1,0:T(8,128)S(1)}) custom-call(bf16[12,49152]{1,0:T(8,128)(2,1)} %coef_hbm.1, s32[3,3072]{1,0:T(4,128)} %expo_hbm.1, f32[384,1536]{1,0:T(8,128)} %bitcast.4, bf16[2,256,384]{2,1,0:T(8,128)(2,1)} %constant.16.clone.spread_hbm, ...), custom_call_target="tpu_custom_call" | custom-call | tf_op jit(solution)/shard_map/exchange/pallas_call | solution.py:498
  40.0 2.2 %deliver.1 = (f32[384,1536]{1,0:T(8,128)}, f32[384,1536]{1,0:T(8,128)}, f32[1,1]{1,0:T(1,128)}) custom-call(f32[384,1536]{1,0:T(8,128)S(1)} %get-tuple-element.9.dec_ref, f32[384,1536]{1,0:T(8,128)S(1)} %get-tuple-element.10.res_ref, f32[8,128]{1,0:T(8,128)S(1)} %get-tuple-element.11.sum_ref), custom_call_target="tpu_custom_call" | custom-call | tf_op jit(solution)/shard_map/deliver/pallas_call | solution.py:526

commit v7 on v6

--- a/solution.py
+++ b/solution.py
@@ -187,16 +187,26 @@
     second = [load(6, edge_hbm, edge), load(7, part_hbm, part_of), load(8, turn_hbm, turn)]
     third = [load(9, left_hbm, left), load(10, depth_hbm, depth), load(11, place_hbm, place)]
     third += [load(12, lift_hbm, lift), load(13, right_hbm, right)]
-    for copy in [*first, *chunks, *second]:
-        copy.start()
 
     entry = pltpu.get_barrier_semaphore()
-    def everywhere(act):
-        for distance in sorted(sum(orders(), []), key=lambda d: -sum(min(v, 4 - v) for v in d[:3])):
-            act(ident(peers.at(*distance)))
+    def hops(distance):
+        return sum(min(v, 4 - v) for v in distance[:3])
+
+    def everywhere(act, least=0, most=6):
+        for distance in sorted(sum(orders(), []), key=lambda d: -hops(d)):
+            if least <= hops(distance) <= most:
+                act(ident(peers.at(*distance)))
+
+    def greet(there):
+        pl.semaphore_signal(entry, inc=1, device_id=there, device_id_type=MESH)
 
     with jax.named_scope("s_signal"):
-        everywhere(lambda there: pl.semaphore_signal(entry, inc=1, device_id=there, device_id_type=MESH))
+        everywhere(greet, 5, 6)
+        for copy in [*first, *chunks]:
+            copy.start()
+        everywhere(greet, 0, 4)
+        for copy in second:
+            copy.start()
 
     def clear(g, _):
         sbuf[pl.ds(g * 16, 16), 8:16, :] = jnp.zeros((16, 8, CELLS), BF16)

time: 42.4 us -> 42.4 us (level)
  no operation moved by 1% of the time
where the time goes in v7:
time: 42.4 us; the launch traced here: 42.2 us
  Pallas kernels  41.6 us (98%)
  between operations  0.64 us (2%)
    pallas_call x1, Pallas kernels, shards(): pl.pallas_call(kernel, name='exchange', out_shape=(field, field, jax.Shap...  39.4 us
    pallas_call x1, Pallas kernels, shards(): pl.pallas_call(deliver, name='deliver', out_shape=(field, field, jax.Shap...  2.21 us

profile of v7, /device:TPU:1, one launch (start us, length us, event | category | flops | bytes accessed | tf_op | source)
XLA Modules:
  0.0 42.2 jit_solution(2152486672229237334)
XLA Ops:
  0.6 39.4 %exchange.1 = (f32[384,1536]{1,0:T(8,128)S(1)}, f32[384,1536]{1,0:T(8,128)S(1)}, f32[8,128]{1,0:T(8,128)S(1)}) custom-call(bf16[12,49152]{1,0:T(8,128)(2,1)} %coef_hbm.1, s32[3,3072]{1,0:T(4,128)} %expo_hbm.1, f32[384,1536]{1,0:T(8,128)} %bitcast.4, bf16[2,256,384]{2,1,0:T(8,128)(2,1)} %constant.16.clone.spread_hbm, ...), custom_call_target="tpu_custom_call" | custom-call | tf_op jit(solution)/shard_map/exchange/pallas_call | solution.py:508
  40.0 2.2 %deliver.1 = (f32[384,1536]{1,0:T(8,128)}, f32[384,1536]{1,0:T(8,128)}, f32[1,1]{1,0:T(1,128)}) custom-call(f32[384,1536]{1,0:T(8,128)S(1)} %get-tuple-element.9.dec_ref, f32[384,1536]{1,0:T(8,128)S(1)} %get-tuple-element.10.res_ref, f32[8,128]{1,0:T(8,128)S(1)} %get-tuple-element.11.sum_ref), custom_call_target="tpu_custom_call" | custom-call | tf_op jit(solution)/shard_map/deliver/pallas_call | solution.py:536
